TPU v7x, 32 devices: a whole 2x2x4 slice. The times are simulated.
32 devices in a mesh: lat: 4 (over y, x), lon: 8 (over z, core).
Axes of the slice: x: 2, y: 2, z: 4, core: 2. Of those that a mesh axis runs over, the one named last changes fastest.
Arguments:
- block_input: float32 [96, 192, 384], P('lat', 'lon'), may hold values from -90 to 90, as said below
- cotangent: float32 [96, 192, 384], P('lat', 'lon'), may hold values from -6 to 6
- weights: float32 [1769472], replicated, may hold values from -4 to 4, as said below
- first_moment: float32 [1769472], P(('lat', 'lon')), may hold values from -3 to 3
- second_moment: float32 [1769472], P(('lat', 'lon')), may hold values from 0.05 to 2
- bias_table: float32 [12, 529], replicated, may hold values from -5 to 5
- bias_index: int32 [144, 144], replicated, may hold values from 0 to 528
- region_ids: int32 [96, 192], P('lat', 'lon'), may hold values from 0 to 2
Outputs:
- grad_input: float32 [96, 192, 384], P('lat', 'lon')
- weights_new: float32 [1769472], replicated
- first_new: float32 [1769472], P(('lat', 'lon'))
- second_new: float32 [1769472], P(('lat', 'lon'))
- table_grad: float32 [12, 529], replicated
Inputs may be any that keep to these rules, and one draw needn't show every extreme that they name: `block_input`: Tokens' features; real values. `weights`: real values. `region_ids`: entry (r, c) is the region of the token at ((r + 6) mod 96, (c + 6) mod 192) of the input grid.
All inputs are finite; a program needn't handle non-finite values.
Results may differ from a plain program's by a relative error of at most 0.0003.
Values sent between devices are 32-bit elements; how exact they have to be, the bound alone decides.
A program may use at most 128 MiB of HBM per device.

v0:
```python
import functools
import math

import jax
import jax.numpy as jnp
from jax import lax
from jax.experimental import pallas as pl
from jax.experimental.pallas import tpu as pltpu
from jax.sharding import PartitionSpec as P

D = 384
HEADS = 12
FF = 1536
WIN = 12
HEAD_DIM = 32
SHIFT = 6
TOK = WIN * WIN
LOW = 32
HEAD_ROWS = 16
LANES = 128
CHUNKS = 4

high = lax.Precision.HIGH
F32 = jnp.float32
BF16 = jnp.bfloat16
NN = (((1,), (0,)), ((), ()))
NT = (((1,), (1,)), ((), ()))
TN = (((0,), (0,)), ((), ()))


def passed_along(value, axis, by):
    size = lax.axis_size(axis)
    return lax.ppermute(value, axis, [(i, (i + by) % size) for i in range(size)])


def windows(tensor):
    height, breadth, features = tensor.shape
    blocks = tensor.reshape(height // WIN, WIN, breadth // WIN, WIN, features)
    return blocks.transpose(0, 2, 1, 3, 4).reshape(-1, WIN * WIN, features)


def unwindow(blocks, height, breadth):
    features = blocks.shape[-1]
    tensor = blocks.reshape(height // WIN, breadth // WIN, WIN, WIN, features)
    return tensor.transpose(0, 2, 1, 3, 4).reshape(height, breadth, features)


def unpack(packed):
    first_cut = D * 3 * D
    second_cut = first_cut + D * D
    third_cut = second_cut + D * FF
    return (
        packed[:first_cut].reshape(D, 3 * D),
        packed[first_cut:second_cut].reshape(D, D),
        packed[second_cut:third_cut].reshape(D, FF),
        packed[third_cut:].reshape(FF, D),
    )


def split(value):
    upper = value.astype(BF16)
    return upper, (value - upper.astype(F32)).astype(BF16)


def mul(a, b, dims):
    return lax.dot_general(a, b, dims, preferred_element_type=F32)


def dot3(a, b, dims):
    return mul(a[0], b[0], dims) + mul(a[0], b[1], dims) + mul(a[1], b[0], dims)


def head_of(pair, h):
    at = h * HEAD_DIM
    return pair[0][:, at : at + HEAD_DIM], pair[1][:, at : at + HEAD_DIM]


def attention_forward_kernel(qkv_ref, bias_ref, row_ref, col_ref, context_ref, prob_ref):
    q = split(qkv_ref[0, :, :D] * (1.0 / math.sqrt(HEAD_DIM)))
    k = split(qkv_ref[0, :, D : 2 * D])
    v = split(qkv_ref[0, :, 2 * D :])
    allowed = col_ref[0] == row_ref[0]
    parts = []
    for h in range(HEADS):
        scores = dot3(head_of(q, h), head_of(k, h), NT) + bias_ref[h]
        masked = jnp.where(allowed, scores, -jnp.inf)
        raised = jnp.exp(masked - jnp.max(masked, axis=-1, keepdims=True))
        prob = raised / jnp.sum(raised, axis=-1, keepdims=True)
        prob_ref[0, h] = prob
        parts.append(dot3(split(prob), head_of(v, h), NN))
    context_ref[0] = jnp.concatenate(parts, axis=1)


def attention_backward_kernel(qkv_ref, prob_ref, grad_ref, dqkv_ref, dbias_ref):
    @pl.when(pl.program_id(0) == 0)
    def _():
        dbias_ref[...] = jnp.zeros_like(dbias_ref)

    scale = 1.0 / math.sqrt(HEAD_DIM)
    q = split(qkv_ref[0, :, :D])
    k = split(qkv_ref[0, :, D : 2 * D])
    v = split(qkv_ref[0, :, 2 * D :])
    g = split(grad_ref[0])
    dq, dk, dv = [], [], []
    for h in range(HEADS):
        prob = prob_ref[0, h]
        g_h = head_of(g, h)
        dv.append(dot3(split(prob), g_h, TN))
        dprob = dot3(g_h, head_of(v, h), NT)
        dscore = prob * (dprob - jnp.sum(prob * dprob, axis=-1, keepdims=True))
        dbias_ref[h] += dscore
        dscore = split(dscore * scale)
        dq.append(dot3(dscore, head_of(k, h), NN))
        dk.append(dot3(dscore, head_of(q, h), TN))
    dqkv_ref[0] = jnp.concatenate(dq + dk + dv, axis=1)


def bias_kernel(levels, table_ref, index_ref, bias_ref):
    upper, lower = split(table_ref[...])
    rows = lax.broadcasted_iota(jnp.int32, (LOW, TOK), 0)
    for r in range(index_ref.shape[0]):
        index = index_ref[r : r + 1, :]
        low = index & (LOW - 1)
        high_part = index >> 5
        hot = jnp.where(rows == low, 1.0, 0.0).astype(BF16)
        spread = mul(upper, hot, NN) + mul(lower, hot, NN)
        total = jnp.zeros((HEAD_ROWS, TOK), F32)
        for level in range(levels):
            total = jnp.where(
                high_part == level, spread[level * HEAD_ROWS : (level + 1) * HEAD_ROWS], total
            )
        bias_ref[:, r, :] = total[:HEADS]


def table_kernel(levels, grad_ref, index_ref, table_ref):
    @pl.when(pl.program_id(0) == 0)
    def _():
        table_ref[...] = jnp.zeros_like(table_ref)

    rows = lax.broadcasted_iota(jnp.int32, (LOW, TOK), 0)
    for r in range(index_ref.shape[0]):
        index = index_ref[r : r + 1, :]
        low = index & (LOW - 1)
        high_part = index >> 5
        hot = jnp.where(rows == low, 1.0, 0.0).astype(BF16)
        grad = jnp.concatenate(
            [grad_ref[:, r, :], jnp.zeros((HEAD_ROWS - HEADS, TOK), F32)], axis=0
        )
        stacked = jnp.concatenate(
            [jnp.where(high_part == level, grad, 0.0) for level in range(levels)], axis=0
        )
        upper, lower = split(stacked)
        table_ref[...] += mul(upper, hot, NT) + mul(lower, hot, NT)


def attention_forward(qkv, bias, row_label, col_label):
    count = qkv.shape[0]
    return pl.pallas_call(
        attention_forward_kernel,
        grid=(count,),
        in_specs=[
            pl.BlockSpec((1, TOK, 3 * D), lambda w: (w, 0, 0)),
            pl.BlockSpec((HEADS, TOK, TOK), lambda w: (0, 0, 0)),
            pl.BlockSpec((1, 1, TOK), lambda w: (w, 0, 0)),
            pl.BlockSpec((1, TOK, 1), lambda w: (w, 0, 0)),
        ],
        out_specs=(
            pl.BlockSpec((1, TOK, D), lambda w: (w, 0, 0)),
            pl.BlockSpec((1, HEADS, TOK, TOK), lambda w: (w, 0, 0, 0)),
        ),
        out_shape=(
            jax.ShapeDtypeStruct((count, TOK, D), F32),
            jax.ShapeDtypeStruct((count, HEADS, TOK, TOK), F32),
        ),
        cost_estimate=pl.CostEstimate(
            flops=40000000 * count, bytes_accessed=4000000 * count, transcendentals=250000 * count
        ),
    )(qkv, bias, row_label, col_label)


def attention_backward(qkv, prob, grad):
    count = qkv.shape[0]
    return pl.pallas_call(
        attention_backward_kernel,
        grid=(count,),
        in_specs=[
            pl.BlockSpec((1, TOK, 3 * D), lambda w: (w, 0, 0)),
            pl.BlockSpec((1, HEADS, TOK, TOK), lambda w: (w, 0, 0, 0)),
            pl.BlockSpec((1, TOK, D), lambda w: (w, 0, 0)),
        ],
        out_specs=(
            pl.BlockSpec((1, TOK, 3 * D), lambda w: (w, 0, 0)),
            pl.BlockSpec((HEADS, TOK, TOK), lambda w: (0, 0, 0)),
        ),
        out_shape=(
            jax.ShapeDtypeStruct((count, TOK, 3 * D), F32),
            jax.ShapeDtypeStruct((HEADS, TOK, TOK), F32),
        ),
        cost_estimate=pl.CostEstimate(
            flops=80000000 * count, bytes_accessed=4000000 * count, transcendentals=0
        ),
    )(qkv, prob, grad)


def look_up(table, index):
    entries = table.shape[1]
    levels = -(-entries // LOW)
    padded = jnp.pad(table, ((0, HEAD_ROWS - HEADS), (0, levels * LOW - entries)))
    padded = padded.reshape(HEAD_ROWS, levels, LOW).transpose(1, 0, 2).reshape(-1, LOW)
    return pl.pallas_call(
        functools.partial(bias_kernel, levels),
        grid=(TOK // 8,),
        in_specs=[
            pl.BlockSpec((levels * HEAD_ROWS, LOW), lambda i: (0, 0)),
            pl.BlockSpec((8, TOK), lambda i: (i, 0)),
        ],
        out_specs=pl.BlockSpec((HEADS, 8, TOK), lambda i: (0, i, 0)),
        out_shape=jax.ShapeDtypeStruct((HEADS, TOK, TOK), F32),
        cost_estimate=pl.CostEstimate(flops=1000000000, bytes_accessed=2000000, transcendentals=0),
    )(padded, index)


def table_gradient(grad, index, entries):
    levels = -(-entries // LOW)
    stacked = pl.pallas_call(
        functools.partial(table_kernel, levels),
        grid=(TOK // 8,),
        in_specs=[
            pl.BlockSpec((HEADS, 8, TOK), lambda i: (0, i, 0)),
            pl.BlockSpec((8, TOK), lambda i: (i, 0)),
        ],
        out_specs=pl.BlockSpec((levels * HEAD_ROWS, LOW), lambda i: (0, 0)),
        out_shape=jax.ShapeDtypeStruct((levels * HEAD_ROWS, LOW), F32),
        cost_estimate=pl.CostEstimate(flops=1000000000, bytes_accessed=2000000, transcendentals=0),
    )(grad, index)
    return stacked


def unstack_table(stacked, entries):
    levels = -(-entries // LOW)
    table = stacked.reshape(levels, HEAD_ROWS, LOW).transpose(1, 0, 2)
    return table.reshape(HEAD_ROWS, levels * LOW)[:HEADS, :entries]


def bit_count(size):
    return size.bit_length() - 1


def exchange_kernel(lat_bits, lon_bits, chunks, factor, grad_ref, table_ref, weight_ref, first_ref,
                    second_ref, new_ref, first_out, second_out, table_out, *scratch):
    bits = lat_bits + lon_bits
    lat, lon = lax.axis_index("lat"), lax.axis_index("lon")
    mine, partner = [], []
    for b in range(bits):
        if b < lat_bits:
            step = 1 << (lat_bits - 1 - b)
            bit = lax.rem(lat // step, 2)
            partner.append({"lat": lat + step * (1 - 2 * bit), "lon": lon})
        else:
            step = 1 << (bits - 1 - b)
            bit = lax.rem(lon // step, 2)
            partner.append({"lat": lat, "lon": lon + step * (1 - 2 * bit)})
        mine.append(bit)
    core, inner = bits - 1, list(range(lat_bits, bits - 1))[::-1]
    ahead, back = list(range(lat_bits))[::-1], list(range(lat_bits))
    orders = [[core] + (ahead if i % 2 == 0 else back) + inner for i in range(len(chunks))]
    held = [scratch[i * bits : (i + 1) * bits] for i in range(len(chunks))]
    table_held = scratch[len(chunks) * bits]
    own_weight, rs_send, rs_recv, ag_send, ag_recv, t_send, t_recv, w_sem = scratch[len(chunks) * bits + 1 :]

    barrier = pltpu.get_barrier_semaphore()
    for b in range(bits):
        pl.semaphore_signal(barrier, inc=1, device_id=partner[b], device_id_type=pl.DeviceIdType.MESH)
    pl.semaphore_wait(barrier, bits)

    def copy(src, dst, send, recv, b):
        return pltpu.make_async_remote_copy(
            src_ref=src, dst_ref=dst, send_sem=send, recv_sem=recv,
            device_id=partner[b], device_id_type=pl.DeviceIdType.MESH)

    def select(dims, b, value):
        return tuple(value if d == b else slice(None) for d in dims)

    def reduce_copy(i, s):
        order, (start, rows) = orders[i], chunks[i]
        b = order[s]
        dims = sorted(order[s:])
        if s == 0:
            src = grad_ref.at[select(dims, b, 1 - mine[b]) + (pl.ds(start, rows),)]
        else:
            src = held[i][s - 1].at[select(dims, b, 1 - mine[b])]
        return copy(src, held[i][s], rs_send.at[i, s], rs_recv.at[i, s], b)

    def reduce_add(i, s):
        order, (start, rows) = orders[i], chunks[i]
        b = order[s]
        dims = sorted(order[s:])
        if s == 0:
            kept = grad_ref[select(dims, b, mine[b]) + (pl.ds(start, rows),)]
        else:
            kept = held[i][s - 1][select(dims, b, mine[b])]
        held[i][s][...] += kept

    def gather_copy(i, s):
        order, (start, rows) = orders[i], chunks[i]
        known = set(order[s + 1 :])
        index = tuple(slice(None) if d in known else mine[d] for d in range(bits))
        region = new_ref.at[index + (pl.ds(start, rows),)]
        return copy(region, region, ag_send.at[i, s], ag_recv.at[i, s], order[s])

    def table_copy(s):
        return copy(table_out if s else table_ref, table_held.at[s], t_send.at[s], t_recv.at[s], orders[0][s])

    fetch = pltpu.make_async_copy(weight_ref.at[tuple(mine)], own_weight, w_sem)
    fetch.start()
    n = len(chunks)
    live = {}
    for i in range(n):
        live[i] = reduce_copy(i, 0)
        live[i].start()
    table_live = table_copy(0)
    table_live.start()
    for s in range(bits):
        for i in range(n):
            live[i].wait()
            reduce_add(i, s)
            if s + 1 < bits:
                live[i] = reduce_copy(i, s + 1)
                live[i].start()
            else:
                if i == 0:
                    fetch.wait()
                rows = pl.ds(*chunks[i])
                grad = held[i][s][...] * factor
                first = 0.9 * first_ref[rows] + 0.1 * grad
                second = 0.95 * second_ref[rows] + 0.05 * grad * grad
                first_out[rows] = first
                second_out[rows] = second
                new_ref[tuple(mine) + (rows,)] = own_weight[rows] - 0.01 * first / (jnp.sqrt(second) + 1e-08)
                live[i] = gather_copy(i, s)
                live[i].start()
        table_live.wait()
        if s == 0:
            table_out[...] = table_ref[...] + table_held[s]
        else:
            table_out[...] += table_held[s]
        if s + 1 < bits:
            table_live = table_copy(s + 1)
            table_live.start()
    table_out[...] *= factor
    for s in reversed(range(bits)):
        for i in range(n):
            live[i].wait()
            if s > 0:
                live[i] = gather_copy(i, s - 1)
                live[i].start()


def chunk_rows(rows, count):
    groups = -(-rows // 8)
    edges = [min(8 * (groups * i // count), rows) for i in range(count)] + [rows]
    return [(a, b - a) for a, b in zip(edges, edges[1:])]


def reduce_update_gather(grads, table, weights, first, second, factor):
    lat_bits, lon_bits = bit_count(lax.axis_size("lat")), bit_count(lax.axis_size("lon"))
    bits = lat_bits + lon_bits
    rows = first.shape[0] // LANES
    chunks = chunk_rows(rows, CHUNKS)
    split_shape = (2,) * bits + (rows, LANES)
    held = [
        pltpu.VMEM((2,) * (bits - 1 - s) + (count, LANES), F32)
        for _, count in chunks
        for s in range(bits)
    ]
    vmem = pl.BlockSpec(memory_space=pltpu.VMEM)
    shard = jax.ShapeDtypeStruct((rows, LANES), F32)
    dma = pltpu.SemaphoreType.DMA
    new, first_new, second_new, table_sum = pl.pallas_call(
        functools.partial(exchange_kernel, lat_bits, lon_bits, chunks, factor),
        in_specs=[vmem, vmem, pl.BlockSpec(memory_space=pl.ANY), vmem, vmem],
        out_specs=[vmem] * 4,
        out_shape=[jax.ShapeDtypeStruct(split_shape, F32), shard, shard,
                   jax.ShapeDtypeStruct(table.shape, F32)],
        scratch_shapes=held + [
            pltpu.VMEM((bits,) + table.shape, F32),
            pltpu.VMEM((rows, LANES), F32),
            dma((len(chunks), bits)), dma((len(chunks), bits)),
            dma((len(chunks), bits)), dma((len(chunks), bits)),
            dma((bits,)), dma((bits,)), dma(()),
        ],
        compiler_params=pltpu.CompilerParams(
            collective_id=0, has_side_effects=True, vmem_limit_bytes=56 * 1024 * 1024),
    )(grads.reshape(split_shape), table, weights.reshape(split_shape),
      first.reshape(rows, LANES), second.reshape(rows, LANES))
    return new.reshape(-1), first_new.reshape(-1), second_new.reshape(-1), table_sum


def shift_ahead(stacked):
    from_east = passed_along(stacked[:, :, :SHIFT], "lon", -1)
    widened = jnp.concatenate([stacked[:, :, SHIFT:], from_east], axis=2)
    from_south = passed_along(widened[:, :SHIFT], "lat", -1)
    return jnp.concatenate([widened[:, SHIFT:], from_south], axis=1)


def shift_back(stacked):
    from_north = passed_along(stacked[:, -SHIFT:], "lat", 1)
    lengthened = jnp.concatenate([from_north, stacked[:, :-SHIFT]], axis=1)
    from_west = passed_along(lengthened[:, :, -SHIFT:], "lon", 1)
    return jnp.concatenate([from_west, lengthened[:, :, :-SHIFT]], axis=2)


def dense(a, b, dims):
    return lax.dot_general(a, b, dims, precision=high, preferred_element_type=F32)


def normalize(values):
    center = values - jnp.mean(values, axis=-1, keepdims=True)
    spread = jnp.mean(center * center, axis=-1, keepdims=True)
    inverse = 1.0 / jnp.sqrt(spread + 1e-05)
    return center * inverse, inverse


def normalize_backward(grad, normed, inverse):
    return inverse * (
        grad
        - jnp.mean(grad, axis=-1, keepdims=True)
        - normed * jnp.mean(grad * normed, axis=-1, keepdims=True)
    )


def per_device(
    block_input, cotangent, weights, first_moment, second_moment, bias_table, bias_index, region_ids
):
    tile_rows, tile_cols, _ = block_input.shape
    lat_count = lax.axis_size("lat")
    lon_count = lax.axis_size("lon")
    tokens = tile_rows * tile_cols
    entries = bias_table.shape[1]
    global_rows = lax.axis_index("lat") * tile_rows + jnp.arange(tile_rows)
    wrapped = global_rows >= tile_rows * lat_count - SHIFT
    labels = region_ids * 2 + wrapped[:, None].astype(jnp.int32)
    labels = windows(labels[:, :, None])[:, :, 0]

    bias = look_up(bias_table, bias_index)
    w_qkv, w_proj, w_up, w_down = unpack(weights)

    moved = shift_ahead(jnp.stack([block_input, cotangent]))
    x = windows(moved[0]).reshape(tokens, D)
    ct = windows(moved[1]).reshape(tokens, D)

    x_normed, x_inverse = normalize(x)
    qkv = dense(x_normed, w_qkv, NN).reshape(-1, TOK, 3 * D)
    context, prob = attention_forward(qkv, bias, labels[:, None, :], labels[:, :, None])
    context = context.reshape(tokens, D)
    mixed = x + dense(context, w_proj, NN)
    m_normed, m_inverse = normalize(mixed)
    hidden, gelu_back = jax.vjp(
        functools.partial(jax.nn.gelu, approximate=True), dense(m_normed, w_up, NN)
    )
    grad_down = dense(hidden, ct, TN)
    (d_up,) = gelu_back(dense(ct, w_down, NT))
    grad_up = dense(m_normed, d_up, TN)
    d_mixed = ct + normalize_backward(dense(d_up, w_up, NT), m_normed, m_inverse)
    grad_proj = dense(context, d_mixed, TN)
    d_context = dense(d_mixed, w_proj, NT).reshape(-1, TOK, D)
    d_qkv, d_bias = attention_backward(qkv, prob, d_context)
    d_qkv = d_qkv.reshape(tokens, 3 * D)
    grad_qkv = dense(x_normed, d_qkv, TN)
    grad_weights = jnp.concatenate(
        [g.reshape(-1) for g in (grad_qkv, grad_proj, grad_up, grad_down)]
    )

    factor = 1.0 / math.sqrt(tokens * lat_count * lon_count)
    dx = d_mixed + normalize_backward(dense(d_qkv, w_qkv, NT), x_normed, x_inverse)
    dx = unwindow(dx.reshape(-1, TOK, D), tile_rows, tile_cols)
    grad_input = shift_back(dx[None])[0]
    table = table_gradient(d_bias, bias_index, entries)
    gathered, first_new, second_new, table = reduce_update_gather(
        grad_weights, table.reshape(-1, LANES), weights, first_moment, second_moment, factor
    )
    table_grad = unstack_table(table.reshape(-1, LOW), entries)
    return (grad_input, gathered, first_new, second_new, table_grad)


def solution(mesh):
    placed = (
        P("lat", "lon", None),
        P("lat", "lon", None),
        P(),
        P(("lat", "lon")),
        P(("lat", "lon")),
        P(),
        P(),
        P("lat", "lon"),
    )
    return jax.shard_map(
        per_device,
        mesh=mesh,
        in_specs=placed,
        out_specs=(P("lat", "lon", None), P(), P(("lat", "lon")), P(("lat", "lon")), P()),
        check_vma=False,
    )
```

profile of v0, /device:TPU:0, one launch (start us, length us, event | category | flops | bytes accessed | tf_op | source)
XLA Modules:
  0.0 330.5 jit_solution(5617417705275361374)
XLA Ops:
  0.6 1.8 copy_bitcast_fusion
  2.5 4.6 %collective-permute-start = (f32[2,24,6,384]{3,1,2,0:T(8,128)S(1)}, f32[2,24,6,384]{3,1,2,0:T(8,128)S(1)}, u32[]{:S(2)}, u32[]{:S(2)}) collective-permute-start(f32[2,24,6,384]{3,1,2,0:T(8,128)S(1)} %pad_maximum_fusion.4), channel_id=1, source_target_pairs={{0,7},{1,0},{2,1},{3,2},{4,3},{5,4},{6,5},{7,6},{8,15},{9,8},{10,9... | collective-permute-start | bytes 1327112 | tf_op jit(solution)/shard_map/ppermute | solution.py:33
  7.0 4.9 %fusion.33 = (f32[589824]{0:T(1024)}, f32[589824]{0:T(1024)}) fusion(f32[1769472]{0:T(1024)} %param.10), kind=kLoop, calls=%fused_computation.71 | loop fusion | bytes 9437184 | tf_op jit(solution)/shard_map/slice | solution.py:56
  13.3 2.5 collective-permute-start.1
  17.5 1.1 slice.93
  20.6 1.6 slice.91
  22.2 1.6 reshape.218
  23.8 1.6 slice.92
  26.1 3.7 %slice.96 = f32[1536,384]{1,0:T(8,128)} reshape(f32[589824]{0:T(1024)} %get-tuple-element.25) | data formatting | bytes 4718592 | tf_op jit(solution)/shard_map/slice | solution.py:56
  29.8 2.4 slice.98
  32.2 15.0 %shard_map.119.bias_ref = f32[12,144,144]{2,1,0:T(8,128)} custom-call(f32[272,32]{1,0:T(8,128)} %bitcast.79, s32[144,144]{1,0:T(8,128)} %index_ref.3), custom_call_target="tpu_custom_call" | custom-call | flops 1000000000 | bytes 2000000 | tf_op jit(solution)/shard_map/pallas_call | solution.py:210
  47.2 1.5 slice_maximum_fusion
  48.7 1.1 copy.58
  49.8 1.1 pad_maximum_fusion.2
  52.0 1.3 reshape_squeeze.7
  57.5 1.4 copy.64
  60.5 2.1 subtract_multiply_fusion
  62.6 1.4 copy.63
  63.9 1.2 copy.62
  66.7 2.9 reshape_reshape.16
  69.5 2.2 copy.59
  71.8 1.3 reshape_squeeze.6
  73.0 1.1 copy.60
  74.2 2.3 reshape_reshape.14
  76.5 1.4 reshape_reshape.15
  77.9 1.9 subtract_multiply_fusion.2
  79.9 3.9 %fusion.19.qkv_ref = f32[4,144,1152]{2,1,0:T(8,128)} fusion(f32[384,1152,1]{1,0,2:T(8,128)S(1)} %copy-done.6, f32[4,144,384]{2,0,1:T(4,128)S(1)} %subtract_multiply_fusion.2), kind=kOutput, calls=%fused_computation.31 | convolution fusion | flops 1528823808 | bytes 5308416 | tf_op jit(solution)/shard_map/dot_general | solution.py:414
  83.9 21.0 %shard_map.120 = (f32[4,144,384]{2,1,0:T(8,128)}, f32[4,12,144,144]{3,2,1,0:T(8,128)}) custom-call(f32[4,144,1152]{2,1,0:T(8,128)} %fusion.19.qkv_ref, f32[12,144,144]{2,1,0:T(8,128)} %shard_map.119.bias_ref, s32[4,1,144]{2,1,0:T(1,128)} %broadcast_in_dim_squeeze_reshape.8.row_ref, s32[4,144,1]{2,1,0:T(8,128)} %broadcast_in_dim_squeeze_reshape.9.col_ref), custom_call_target="tpu_custom_call" | custom-call | flops 160000000 | bytes 16000000 | tf_op jit(solution)/shard_map/pallas_call | solution.py:158
  104.8 2.4 fusion.34
  107.6 3.1 fusion.22
  110.7 4.8 %fusion.5 = f32[576,1536]{1,0:T(8,128)S(1)} fusion(f32[576,1536]{1,0:T(8,128)S(1)} %fusion.22, f32[576,384]{1,0:T(8,128)S(1)} %copy-done.8, f32[1536,384]{1,0:T(8,128)S(1)} %copy-done.10), kind=kOutput, calls=%fused_computation.8 | convolution fusion | flops 2055241728 | bytes 10321920 | tf_op jit(solution)/shard_map/dot_general | solution.py:414
  115.5 3.3 fusion.32
  118.8 4.8 %fusion.21 = f32[384,1536]{1,0:T(8,128)} fusion(f32[576,1536]{1,0:T(8,128)S(1)} %fusion.5, f32[576,384]{1,0:T(8,128)S(1)} %get-tuple-element.30, f32[576]{0:T(1024)S(1)} %add_rsqrt_fusion.1, f32[576]{0:T(1024)S(1)} %broadcast_multiply_fusion.5), kind=kOutput, calls=%fused_computation.44 | convolution fusion | flops 2038874112 | bytes 6787584 | tf_op jit(solution)/shard_map/dot_general | solution.py:414
  123.6 5.6 %fusion.6 = f32[1536,384]{1,0:T(8,128)} fusion(f32[576,384]{1,0:T(8,128)S(1)} %copy-done.8, f32[576,1536]{1,0:T(8,128)S(1)} %fusion.22), kind=kOutput, calls=%fused_computation.9 | convolution fusion | flops 2045509632 | bytes 6782976 | tf_op jit(solution)/shard_map/dot_general | solution.py:414
  130.3 1.9 fusion.37
  132.2 1.9 fusion.35.grad_ref
  134.1 28.2 %shard_map.121 = (f32[4,144,1152]{2,1,0:T(8,128)}, f32[12,144,144]{2,1,0:T(8,128)}) custom-call(f32[4,144,1152]{2,1,0:T(8,128)} %fusion.19.qkv_ref, f32[4,12,144,144]{3,2,1,0:T(8,128)} %get-tuple-element.14.prob_ref, f32[4,144,384]{2,1,0:T(8,128)} %fusion.35.grad_ref), custom_call_target="tpu_custom_call" | custom-call | flops 320000000 | bytes 16000000 | tf_op jit(solution)/shard_map/pallas_call | solution.py:183
  162.3 4.4 %fusion.31 = (f32[576]{0:T(1024)S(1)}, f32[576]{0:T(1024)S(1)}, f32[576,384]{1,0:T(8,128)S(1)}) fusion(f32[576]{0:T(1024)S(1)} %sqrt.13, f32[576,384]{1,0:T(8,128)S(1)} %copy-done.1, f32[576]{0:T(1024)S(1)} %div.38, f32[576,1152]{1,0:T(8,128)} %bitcast.64, f32[384,1152]{1,0:T(8,128)S(1)} %copy-done.5), kind=kOutput, calls=%fused_computation.69 | convolution fusion | flops 1529928576 | bytes 6202368 | tf_op jit(solution)/shard_map/dot_general | solution.py:414
  169.7 3.2 reshape.208
  173.0 3.3 reshape.207
  176.3 1.9 reshape.206
  178.2 4.9 %fusion.36 = f32[384,1152]{1,0:T(8,128)} fusion(f32[576,384]{1,0:T(8,128)} %mul.157, f32[576,1152]{1,0:T(8,128)S(1)} %bitcast.65), kind=kOutput, calls=%fused_computation.74 | convolution fusion | flops 1528823808 | bytes 5308416 | tf_op jit(solution)/shard_map/dot_general | solution.py:414
  183.1 2.7 reshape.205
  186.5 8.9 %pad_maximum_fusion = f32[1769472]{0:T(1024)} fusion(f32[589824]{0:T(1024)S(1)} %copy-done.4, f32[589824]{0:T(1024)} %reshape.207, f32[147456]{0:T(1024)} %reshape.206, f32[442368]{0:T(1024)} %reshape.205), kind=kLoop, calls=%fused_computation | loop fusion | flops 5308416 | bytes 14155776 | tf_op jit(solution)/shard_map/concatenate | solution.py:470
  195.4 16.3 %shard_map.122 = f32[272,32]{1,0:T(8,128)} custom-call(f32[12,144,144]{2,1,0:T(8,128)} %get-tuple-element.16.grad_ref, s32[144,144]{1,0:T(8,128)} %index_ref.3), custom_call_target="tpu_custom_call" | custom-call | flops 1000000000 | bytes 2000000 | tf_op jit(solution)/shard_map/pallas_call | solution.py:225
  211.7 1.6 reshape.210.table_ref
  213.3 107.6 %shard_map.123 = (f32[2,2,2,2,2,432,128]{6,5,4,3,2,1,0:T(8,128)}, f32[432,128]{1,0:T(8,128)}, f32[432,128]{1,0:T(8,128)}, f32[68,128]{1,0:T(8,128)}) custom-call(f32[2,2,2,2,2,432,128]{6,5,4,3,2,1,0:T(8,128)} %bitcast.62, f32[68,128]{1,0:T(8,128)} %reshape.210.table_ref, f32[2,2,2,2,2,432,128]{6,5,4,3,2,1,0:T(8,128)} %bitcast.61, f32[432,128]{1,0:T(8,128)} %bitcast.75, ...), custom_call_target="tpu_custom_call" | custom-call | tf_op jit(solution)/shard_map/pallas_call | solution.py:379
  323.5 5.2 %copy.89 = f32[1769472]{0:T(1024)} copy(f32[1769472]{0:T(1024)} %bitcast.66) | data formatting | bytes 14155776
  (96 shorter events, 23.6 us)
Async XLA Ops:
  2.5 10.4 %collective-permute-start = (f32[2,24,6,384]{3,1,2,0:T(8,128)S(1)}, f32[2,24,6,384]{3,1,2,0:T(8,128)S(1)}, u32[]{:S(2)}, u32[]{:S(2)}) collective-permute-start(f32[2,24,6,384]{3,1,2,0:T(8,128)S(1)} %pad_maximum_fusion.4), channel_id=1, source_target_pairs={{0,7},{1,0},{2,1},{3,2},{4,3},{5,4},{6,5},{7,6},{8,15},{9,8},{10,9... | collective-permute-start | bytes 1327112 | tf_op jit(solution)/shard_map/ppermute | solution.py:33
  11.9 3.9 %copy-start.19 = (s32[24,24]{1,0:T(8,128)S(1)}, s32[24,24]{1,0:T(8,128)}, u32[]{:S(2)}) copy-start(s32[24,24]{1,0:T(8,128)} %param.15) | copy-start | bytes 6916
  12.0 1.2 copy-start.2
  13.3 35.4 %collective-permute-start.1 = (f32[2,6,24,384]{3,2,1,0:T(8,128)S(1)}, f32[2,6,24,384]{3,2,1,0:T(8,128)}, u32[]{:S(2)}, u32[]{:S(2)}) collective-permute-start(f32[2,6,24,384]{3,2,1,0:T(8,128)S(1)} %copy.57), channel_id=1, source_target_pairs={{0,24},{8,0},{16,8},{24,16},{1,25},{9,1},{17,9},{25,17},{2,26},{10... | collective-permute-start | bytes 1327112 | tf_op jit(solution)/shard_map/ppermute | solution.py:33
  23.8 1.6 copy-start.18
  53.5 0.6 copy-start.12
  54.5 0.6 copy-start.15
  74.1 3.7 %copy-start.13 = (f32[4,144]{0,1:T(8,128)S(1)}, f32[4,144]{0,1:T(8,128)}, u32[]{:S(2)}) copy-start(f32[4,144]{0,1:T(8,128)} %copy.65) | copy-start | bytes 6916
  74.2 3.7 %copy-start.14 = (f32[4,144]{0,1:T(8,128)S(1)}, f32[4,144]{0,1:T(8,128)}, u32[]{:S(2)}) copy-start(f32[4,144]{0,1:T(8,128)} %copy.67) | copy-start | bytes 6916
  77.9 27.0 %copy-start = (f32[576,384]{1,0:T(8,128)}, f32[576,384]{1,0:T(8,128)S(1)}, u32[]{:S(2)}) copy-start(f32[576,384]{1,0:T(8,128)S(1)} %reshape_reshape.15) | copy-start | bytes 2654212
  77.9 2.1 copy-start.6
  107.6 3.1 copy-start.8
  107.6 3.1 copy-start.10
  129.1 1.2 copy-start.9
  129.1 3.1 copy-start.11
  134.1 28.2 %copy-start.1 = (f32[576,384]{1,0:T(8,128)S(1)}, f32[576,384]{1,0:T(8,128)}, u32[]{:S(2)}) copy-start(f32[576,384]{1,0:T(8,128)} %copy-done) | copy-start | bytes 2654212
  134.1 28.2 %copy-start.5 = (f32[384,1152]{1,0:T(8,128)S(1)}, f32[384,1152]{1,0:T(8,128)}, u32[]{:S(2)}) copy-start(f32[384,1152]{1,0:T(8,128)} %slice.92) | copy-start | bytes 5308420
  167.3 1.4 copy-start.7
  173.0 5.2 %copy-start.3 = (f32[4,144,1152]{2,1,0:T(8,128)S(1)}, f32[4,144,1152]{2,1,0:T(8,128)}, u32[]{:S(2)}) copy-start(f32[4,144,1152]{2,1,0:T(8,128)} %get-tuple-element.15) | copy-start | bytes 7962628
  178.2 7.6 %collective-permute-start.2 = (f32[1,6,24,384]{3,2,1,0:T(8,128)}, f32[1,6,24,384]{3,2,1,0:T(8,128)S(1)}, u32[]{:S(2)}, u32[]{:S(2)}) collective-permute-start(f32[1,6,24,384]{3,2,1,0:T(8,128)} %slice.110), channel_id=1, source_target_pairs={{0,8},{8,16},{16,24},{24,0},{1,9},{9,17},{17,25},{25,1},{2,10},{10... | collective-permute-start | bytes 663560 | tf_op jit(solution)/shard_map/ppermute | solution.py:33
  183.1 3.4 %copy-start.4 = (f32[589824]{0:T(1024)S(1)}, f32[589824]{0:T(1024)}, u32[]{:S(2)}) copy-start(f32[589824]{0:T(1024)} %reshape.208) | copy-start | bytes 7077892
  186.5 136.0 %collective-permute-start.3 = (f32[1,24,6,384]{3,2,1,0:T(8,128)}, f32[1,24,6,384]{3,2,1,0:T(8,128)S(1)}, u32[]{:S(2)}, u32[]{:S(2)}) collective-permute-start(f32[1,24,6,384]{3,2,1,0:T(8,128)} %pad_maximum_fusion.5), channel_id=1, source_target_pairs={{0,1},{1,2},{2,3},{3,4},{4,5},{5,6},{6,7},{7,0},{8,9},{9,10},{10,1... | collective-permute-start | bytes 663560 | tf_op jit(solution)/shard_map/ppermute | solution.py:33
  323.5 5.2 %copy-start.17 = (f32[432,128]{1,0:T(8,128)S(1)}, f32[432,128]{1,0:T(8,128)}, u32[]{:S(2)}) copy-start(f32[432,128]{1,0:T(8,128)} %get-tuple-element.18) | copy-start | bytes 663556
  323.5 5.9 %copy-start.16 = (f32[432,128]{1,0:T(8,128)S(1)}, f32[432,128]{1,0:T(8,128)}, u32[]{:S(2)}) copy-start(f32[432,128]{1,0:T(8,128)} %get-tuple-element.19) | copy-start | bytes 663556
where the time goes:
time: 336 us; the launch traced here: 330 us
  Pallas kernels  188 us (56%)
  local copies, waits for them, and re-layouts  73.1 us (22%)
  matrix products  41 us (12%)
  other arithmetic  19 us (6%)
  starting transfers between devices  7.07 us (2%)
    pallas_call x1, Pallas kernels, reduce_update_gather(): pl.pallas_call(functools.partial(exchange_kernel, lat_bits, lon_bits, chu...  108 us
    dot_general x11, matrix products, dense(): lax.dot_general(a, b, dims, precision=high, preferred_element_type=F32)  41 us
    pallas_call x1, Pallas kernels, attention_backward(): pl.pallas_call(attention_backward_kernel, grid=(count,), in_specs=[pl.Blo...  28.2 us
    pallas_call x1, Pallas kernels, attention_forward(): pl.pallas_call(attention_forward_kernel, grid=(count,), in_specs=[pl.Bloc...  21 us
    pallas_call x1, Pallas kernels, table_gradient(): pl.pallas_call(functools.partial(table_kernel, levels), grid=(TOK // 8,),...  16.3 us
    pallas_call x1, Pallas kernels, look_up(): pl.pallas_call(functools.partial(bias_kernel, levels), grid=(TOK // 8,),...  15 us
    reshape x4, local copies, waits for them, and re-layouts, per_device(): g.reshape(-1)  11.1 us
    unnamed x43, local copies, waits for them, and re-layouts  9.46 us
  transfers between devices with their start and end apart: 4, of which 1 were waited for; matrix products, arithmetic and copies ran while one was open for 13% of the time, Pallas kernels for 42%

commit v1 on v0

v1 whole, which is shorter than its diff:
```python
import functools
import math

import jax
import jax.numpy as jnp
from jax import lax
from jax.experimental import pallas as pl
from jax.experimental.pallas import tpu as pltpu
from jax.sharding import PartitionSpec as P

D = 384
HEADS = 12
FF = 1536
WIN = 12
HEAD_DIM = 32
SHIFT = 6
TOK = WIN * WIN
HEAD_ROWS = 16
LANES = 128
PACK = LANES // HEAD_DIM
EDGE = 8
FF_BLOCK = 512
CHUNKS = 4
SCALE = 1.0 / math.sqrt(HEAD_DIM)

F32 = jnp.float32
BF16 = jnp.bfloat16
NN = (((1,), (0,)), ((), ()))
NT = (((1,), (1,)), ((), ()))
VMEM_LIMIT = 63 * 1024 * 1024

def split(value):
    upper = value.astype(BF16)
    return upper, (value - upper.astype(F32)).astype(BF16)


def mul(a, b, dims):
    return lax.dot_general(a, b, dims, preferred_element_type=F32)


def dot_nn(a, b):
    return mul(jnp.concatenate([a[0], a[0], a[1]], 1), jnp.concatenate([b[0], b[1], b[0]], 0), NN)


def dot_nt(a, b):
    return mul(jnp.concatenate([a[0], a[0], a[1]], 1), jnp.concatenate([b[0], b[1], b[0]], 1), NT)


def dot_rows(a, b):
    rows = a[0].shape[0]
    both = mul(jnp.concatenate([a[0], a[1]], 0), b[0], NN)
    return both[:rows] + both[rows:] + mul(a[0], b[1], NN)


def dot_cols(a, b):
    cols = b[0].shape[1]
    both = mul(a[0], jnp.concatenate([b[0], b[1]], 1), NN)
    return both[:, :cols] + both[:, cols:] + mul(a[1], b[0], NN)


def normalize(values):
    center = values - jnp.mean(values, axis=-1, keepdims=True)
    spread = jnp.mean(center * center, axis=-1, keepdims=True)
    inverse = 1.0 / jnp.sqrt(spread + 1e-05)
    return center * inverse, inverse


def normalize_backward(grad, normed, inverse):
    return inverse * (
        grad
        - jnp.mean(grad, axis=-1, keepdims=True)
        - normed * jnp.mean(grad * normed, axis=-1, keepdims=True)
    )


def gelu_and_slope(u):
    c = math.sqrt(2.0 / math.pi)
    square = u * u
    t = jnp.tanh(c * u * (1.0 + 0.044715 * square))
    half = 0.5 * (1.0 + t)
    slope = half + 0.5 * u * (1.0 - t * t) * (c * (1.0 + 3.0 * 0.044715 * square))
    return u * half, slope


def window_pieces(height, breadth):
    at = 0
    for r in range(height // WIN):
        for c in range(breadth // WIN):
            for i in range(WIN):
                yield at, SHIFT + r * WIN + i, SHIFT + c * WIN
                at += WIN


def halo_kernel(x_ref, ct_ref, xw_ref, ctw_ref, wide, send, recv, local):
    height, breadth, _ = x_ref.shape
    barrier = pltpu.get_barrier_semaphore()
    for where in neighbours(1):
        pl.semaphore_signal(barrier, inc=1, device_id=where, device_id_type=pl.DeviceIdType.MESH)
    pl.semaphore_wait(barrier, 3)
    copies = []
    for n, ref in enumerate((x_ref, ct_ref)):
        parts = (
            (ref.at[:, pl.ds(0, EDGE)], wide.at[n, pl.ds(0, height), pl.ds(breadth, EDGE)]),
            (ref.at[pl.ds(0, SHIFT)], wide.at[n, pl.ds(height, SHIFT), pl.ds(0, breadth)]),
            (ref.at[pl.ds(0, SHIFT), pl.ds(0, EDGE)],
             wide.at[n, pl.ds(height, SHIFT), pl.ds(breadth, EDGE)]),
        )
        for k, ((src, dst), where) in enumerate(zip(parts, neighbours(-1))):
            copies.append(pltpu.make_async_remote_copy(
                src_ref=src, dst_ref=dst, send_sem=send.at[n, k], recv_sem=recv.at[n, k],
                device_id=where, device_id_type=pl.DeviceIdType.MESH))
        copies.append(pltpu.make_async_copy(
            ref, wide.at[n, pl.ds(0, height), pl.ds(0, breadth)], local.at[n]))
    for copy in copies:
        copy.start()
    for copy in copies:
        copy.wait()
    for n, out in enumerate((xw_ref, ctw_ref)):
        for at, row, col in window_pieces(height, breadth):
            out[at : at + WIN] = wide[n, row, col : col + WIN]


def gather_windows(block_input, cotangent):
    height, breadth, _ = block_input.shape
    dma = pltpu.SemaphoreType.DMA
    return pl.pallas_call(
        halo_kernel,
        in_specs=[pl.BlockSpec(memory_space=pl.ANY)] * 2,
        out_specs=[pl.BlockSpec(memory_space=pltpu.VMEM)] * 2,
        out_shape=[jax.ShapeDtypeStruct((height * breadth, D), F32)] * 2,
        scratch_shapes=[
            pltpu.VMEM((2, height + SHIFT, breadth + EDGE, D), F32),
            dma((2, 3)), dma((2, 3)), dma((2,)),
        ],
        compiler_params=pltpu.CompilerParams(collective_id=1, has_side_effects=True),
    )(block_input, cotangent)


def block_kernel(x_ref, ct_ref, w_ref, table_ref, index_ref, region_ref, grad_ref, edge_ref,
                 table_out, wq, wp, wu, wd, table, index, bias, dbias, prob, xn_s, mn_s, ct_s,
                 qkv_s, q_s, ctx_s, d_s, turned, acc, labels, dqkv_s, spread):
    height, breadth = region_ref.shape
    across = breadth // WIN
    tokens = x_ref.shape[0]
    count = tokens // TOK
    heads, entries = table_ref.shape
    levels = table.shape[1] // LANES
    row_of = [0, D * 3 * D // LANES, (D * 3 * D + D * D) // LANES, (D * 3 * D + D * D + D * FF) // LANES]

    def put(ref, rows, value):
        upper, lower = split(value)
        ref[0, rows], ref[1, rows] = upper, lower

    def pair(ref, *at):
        return ref[(0,) + at], ref[(1,) + at]

    def full(ref):
        return ref[0].astype(F32) + ref[1].astype(F32)

    for dst, start in zip((wq, wp, wu, wd), row_of):
        _, rows, width = dst.shape
        blocks = width // LANES
        for j in range(blocks):
            upper, lower = split(w_ref[pl.ds(start + j, rows, stride=blocks), :])
            dst[0, :, j * LANES : (j + 1) * LANES] = upper
            dst[1, :, j * LANES : (j + 1) * LANES] = lower

    table[...] = jnp.zeros_like(table)
    table[:heads, :entries] = table_ref[...]
    index[...] = jnp.zeros_like(index)
    index[:, :TOK] = index_ref[...]

    def look_up(block, carry):
        rows = pl.ds(pl.multiple_of(block * 8, 8), 8)
        for side in range(2):
            at = index[rows, side * LANES : (side + 1) * LANES]
            low, level_of = at & (LANES - 1), at >> 7
            width = min(LANES, TOK - side * LANES)
            for h in range(heads):
                total = jnp.zeros((8, LANES), F32)
                for level in range(levels):
                    source = jnp.broadcast_to(
                        table[h : h + 1, level * LANES : (level + 1) * LANES], (8, LANES))
                    found = jnp.take_along_axis(source, low, axis=1, mode="promise_in_bounds")
                    total = jnp.where(level_of == level, found, total)
                bias[h, rows, side * LANES : side * LANES + width] = total[:, :width]
        return carry

    lax.fori_loop(0, TOK // 8, look_up, 0)

    lat = lax.axis_index("lat")
    grid_row = lat * height + lax.broadcasted_iota(jnp.int32, (height, breadth), 0)
    wrapped = (grid_row >= height * lax.axis_size("lat") - SHIFT).astype(jnp.int32)
    labels[...] = (region_ref[...] * 2 + wrapped).astype(F32)

    x = x_ref[...]
    x_normed, x_inverse = normalize(x)
    put(xn_s, slice(None), x_normed)
    spread[0] = jnp.broadcast_to(x_inverse, (tokens, LANES))
    qkv = dot_nn(pair(xn_s), pair(wq))
    q = qkv[:, :D] * SCALE
    q_s[...] = q
    for j, part in enumerate((q, qkv[:, D : 2 * D], qkv[:, 2 * D :])):
        upper, lower = split(part)
        qkv_s[0, :, j * D : (j + 1) * D] = upper
        qkv_s[1, :, j * D : (j + 1) * D] = lower
    put(ct_s, slice(None), ct_ref[...])

    lane_head = lax.broadcasted_iota(jnp.int32, (TOK, LANES), 1) >> 5

    def only(head, values):
        keep = lane_head == head
        return tuple(jnp.where(keep, v, jnp.zeros_like(v)) for v in values)

    def tile(which, t, rows):
        cols = slice(which * D + t * LANES, which * D + (t + 1) * LANES)
        return qkv_s[0, rows, cols], qkv_s[1, rows, cols]

    def forward(w, carry):
        rows = pl.ds(pl.multiple_of(w * TOK, TOK), TOK)
        first_row, first_col = (w // across) * WIN, (w % across) * WIN
        position = lax.broadcasted_iota(jnp.int32, (TOK, height), 0)
        quotient = (position * 171) >> 11
        hot = (lax.broadcasted_iota(jnp.int32, (TOK, height), 1) == quotient + first_row).astype(F32)
        picked = mul(hot.astype(BF16), labels[...].astype(BF16), NN)
        position = lax.broadcasted_iota(jnp.int32, (TOK, breadth), 0)
        rest = position - WIN * ((position * 171) >> 11)
        chosen = lax.broadcasted_iota(jnp.int32, (TOK, breadth), 1) == rest + first_col
        label = jnp.sum(jnp.where(chosen, picked, 0.0), axis=1, keepdims=True)
        across_label = jnp.transpose(jnp.broadcast_to(label, (TOK, LANES)))[:1]
        allowed = label == across_label
        for t in range(D // LANES):
            q, k, v = (tile(j, t, rows) for j in range(3))
            total = jnp.zeros((TOK, LANES), F32)
            for head in range(PACK):
                h = t * PACK + head
                scores = dot_nt(only(head, q), k) + bias[h]
                masked = jnp.where(allowed, scores, -jnp.inf)
                raised = jnp.exp(masked - jnp.max(masked, axis=-1, keepdims=True))
                p = split(raised * (1.0 / jnp.sum(raised, axis=-1, keepdims=True)))
                prob[0, w * heads + h], prob[1, w * heads + h] = p
                total += dot_cols(p, only(head, v))
            ctx_s[rows, t * LANES : (t + 1) * LANES] = total
        return carry

    lax.fori_loop(0, count, forward, 0)

    mixed = x_ref[...] + dot_nn(split(ctx_s[...]), pair(wp))
    m_normed, m_inverse = normalize(mixed)
    put(mn_s, slice(None), m_normed)
    spread[1] = jnp.broadcast_to(m_inverse, (tokens, LANES))
    for n, value in enumerate((m_normed, ct_ref[...])):
        turned[n, 0], turned[n, 1] = split(jnp.transpose(value))
    acc[...] = jnp.zeros_like(acc)

    def feed(f, carry):
        cols = pl.ds(pl.multiple_of(f * FF_BLOCK, FF_BLOCK), FF_BLOCK)
        w_up = pair(wu, slice(None), cols)
        hidden, slope = gelu_and_slope(dot_nn(pair(mn_s), w_up))
        d_up = split(dot_nt(pair(ct_s), pair(wd, cols)) * slope)
        hidden = split(hidden)
        blocks = FF // LANES
        grad = dot_rows((turned[0, 0], turned[0, 1]), d_up)
        for j in range(FF_BLOCK // LANES):
            start = row_of[2] + f * (FF_BLOCK // LANES) + j
            grad_ref[pl.ds(start, D, stride=blocks), :] = grad[:, j * LANES : (j + 1) * LANES]
        grad = jnp.transpose(dot_rows((turned[1, 0], turned[1, 1]), hidden))
        blocks = D // LANES
        for j in range(blocks):
            start = row_of[3] + f * (FF_BLOCK * blocks) + j
            grad_ref[pl.ds(start, FF_BLOCK, stride=blocks), :] = grad[:, j * LANES : (j + 1) * LANES]
        acc[...] += dot_nt(d_up, w_up)
        return carry

    lax.fori_loop(0, FF // FF_BLOCK, feed, 0)

    d_mixed = ct_ref[...] + normalize_backward(acc[...], full(mn_s), spread[1][:, :1])
    acc[...] = d_mixed
    d_pair = split(d_mixed)
    turned[0, 0], turned[0, 1] = split(jnp.transpose(ctx_s[...]))
    grad = dot_rows((turned[0, 0], turned[0, 1]), d_pair)
    blocks = D // LANES
    for j in range(blocks):
        grad_ref[pl.ds(row_of[1] + j, D, stride=blocks), :] = grad[:, j * LANES : (j + 1) * LANES]
    d_s[...] = dot_nt(d_pair, pair(wp))
    dbias[...] = jnp.zeros_like(dbias)

    def backward(w, carry):
        rows = pl.ds(pl.multiple_of(w * TOK, TOK), TOK)
        for t in range(D // LANES):
            cols = slice(t * LANES, (t + 1) * LANES)
            k, v = tile(1, t, rows), tile(2, t, rows)
            grad = d_s[rows, cols]
            weighed = grad * ctx_s[rows, cols]
            g = split(grad)
            g_turned = split(jnp.transpose(grad))
            q_turned = split(jnp.transpose(q_s[rows, cols]))
            dq = jnp.zeros((TOK, LANES), F32)
            dk, dv = [], []
            for head in range(PACK):
                h = t * PACK + head
                part = slice(head * HEAD_DIM, (head + 1) * HEAD_DIM)
                upper, lower = prob[0, w * heads + h], prob[1, w * heads + h]
                dprob = dot_nt(only(head, g), v)
                delta = jnp.sum(jnp.where(lane_head == head, weighed, 0.0), axis=-1, keepdims=True)
                dscore = (upper.astype(F32) + lower.astype(F32)) * (dprob - delta)
                dbias[h] += dscore
                ds = split(dscore)
                dq += dot_cols(ds, only(head, k))
                dk.append(dot_rows((q_turned[0][part], q_turned[1][part]), ds))
                dv.append(dot_rows((g_turned[0][part], g_turned[1][part]), (upper, lower)))
            for j, value in enumerate((dq * SCALE, jnp.transpose(jnp.concatenate(dk, 0)),
                                       jnp.transpose(jnp.concatenate(dv, 0)))):
                at = slice(j * D + t * LANES, j * D + (t + 1) * LANES)
                upper, lower = split(value)
                dqkv_s[0, rows, at], dqkv_s[1, rows, at] = upper, lower
        return carry

    lax.fori_loop(0, count, backward, 0)

    x_normed = full(xn_s)
    turned[1, 0], turned[1, 1] = split(jnp.transpose(x_normed))
    grad = dot_rows((turned[1, 0], turned[1, 1]), pair(dqkv_s))
    blocks = 3 * D // LANES
    for j in range(blocks):
        grad_ref[pl.ds(row_of[0] + j, D, stride=blocks), :] = grad[:, j * LANES : (j + 1) * LANES]
    d_normed = dot_nt(pair(dqkv_s), pair(wq))
    q_s[...] = acc[...] + normalize_backward(d_normed, x_normed, spread[0][:, :1])
    edge_ref[...] = jnp.zeros_like(edge_ref)
    for at, row, col in window_pieces(height, breadth):
        edge_ref[row, col : col + WIN] = q_s[at : at + WIN]

    table_acc = jnp.zeros((levels * 2 * HEAD_ROWS, LANES), F32)

    def collect(block, total):
        rows = pl.ds(pl.multiple_of(block * 8, 8), 8)
        at_rows = index_ref[rows, :]
        grads = dbias[:, rows, :]
        for r in range(8):
            at = at_rows[r : r + 1]
            low, level_of = at & (LANES - 1), at >> 7
            grad = jnp.concatenate([grads[:, r, :], jnp.zeros((HEAD_ROWS - heads, TOK), F32)], 0)
            stacked = jnp.concatenate(
                [jnp.where(level_of == level, grad, 0.0) for level in range(levels)], 0)
            hot = (lax.broadcasted_iota(jnp.int32, (LANES, TOK), 0) == low).astype(F32).astype(BF16)
            total = total + mul(jnp.concatenate(split(stacked), 0), hot, NT)
        return total

    total = lax.fori_loop(0, TOK // 8, collect, table_acc)
    table_out[...] = total[: levels * HEAD_ROWS] + total[levels * HEAD_ROWS :]


def block_gradients(x, ct, weights, bias_table, bias_index, region_ids):
    tokens = x.shape[0]
    height, breadth = region_ids.shape
    heads, entries = bias_table.shape
    levels = -(-entries // LANES)
    count = tokens // TOK
    vmem = pl.BlockSpec(memory_space=pltpu.VMEM)
    return pl.pallas_call(
        block_kernel,
        in_specs=[vmem] * 6,
        out_specs=[vmem] * 3,
        out_shape=[
            jax.ShapeDtypeStruct((weights.shape[0] // LANES, LANES), F32),
            jax.ShapeDtypeStruct((height + SHIFT, breadth + EDGE, D), F32),
            jax.ShapeDtypeStruct((levels * HEAD_ROWS, LANES), F32),
        ],
        scratch_shapes=[
            pltpu.VMEM((2, D, 3 * D), BF16),
            pltpu.VMEM((2, D, D), BF16),
            pltpu.VMEM((2, D, FF), BF16),
            pltpu.VMEM((2, FF, D), BF16),
            pltpu.VMEM((HEAD_ROWS, levels * LANES), F32),
            pltpu.VMEM((TOK, 2 * LANES), jnp.int32),
            pltpu.VMEM((heads, TOK, TOK), F32),
            pltpu.VMEM((heads, TOK, TOK), F32),
            pltpu.VMEM((2, count * heads, TOK, TOK), BF16),
            pltpu.VMEM((2, tokens, D), BF16),
            pltpu.VMEM((2, tokens, D), BF16),
            pltpu.VMEM((2, tokens, D), BF16),
            pltpu.VMEM((2, tokens, 3 * D), BF16),
            pltpu.VMEM((tokens, D), F32),
            pltpu.VMEM((tokens, D), F32),
            pltpu.VMEM((tokens, D), F32),
            pltpu.VMEM((2, 2, D, tokens), BF16),
            pltpu.VMEM((tokens, D), F32),
            pltpu.VMEM((height, breadth), F32),
            pltpu.VMEM((2, tokens, 3 * D), BF16),
            pltpu.VMEM((2, tokens, LANES), F32),
        ],
        compiler_params=pltpu.CompilerParams(vmem_limit_bytes=VMEM_LIMIT),
    )(x, ct, weights.reshape(-1, LANES), bias_table, bias_index, region_ids)


def bit_count(size):
    return size.bit_length() - 1


def neighbours(by):
    lat_size, lon_size = lax.axis_size("lat"), lax.axis_size("lon")
    lat = lax.rem(lax.axis_index("lat") + by + lat_size, lat_size)
    lon = lax.rem(lax.axis_index("lon") + by + lon_size, lon_size)
    return ({"lon": lon}, {"lat": lat}, {"lat": lat, "lon": lon})


def exchange_kernel(lat_bits, lon_bits, chunks, factor, grad_ref, table_ref, edge_ref, weight_ref,
                    first_ref, second_ref, new_ref, first_out, second_out, table_final, dx_out, *scratch):
    bits = lat_bits + lon_bits
    lat, lon = lax.axis_index("lat"), lax.axis_index("lon")
    mine, partner = [], []
    for b in range(bits):
        if b < lat_bits:
            step = 1 << (lat_bits - 1 - b)
            bit = lax.rem(lat // step, 2)
            partner.append({"lat": lat + step * (1 - 2 * bit), "lon": lon})
        else:
            step = 1 << (bits - 1 - b)
            bit = lax.rem(lon // step, 2)
            partner.append({"lat": lat, "lon": lon + step * (1 - 2 * bit)})
        mine.append(bit)
    core, inner = bits - 1, list(range(lat_bits, bits - 1))[::-1]
    ahead, back = list(range(lat_bits))[::-1], list(range(lat_bits))
    orders = [[core] + (ahead if i % 2 == 0 else back) + inner for i in range(len(chunks))]
    held = [scratch[i * bits : (i + 1) * bits] for i in range(len(chunks))]
    table_held, table_out = scratch[len(chunks) * bits : len(chunks) * bits + 2]
    west_in, north_in, corner_in, own_weight, rs_send, rs_recv, ag_send, ag_recv, t_send, t_recv, e_send, e_recv, w_sem = scratch[
        len(chunks) * bits + 2 :
    ]

    barrier = pltpu.get_barrier_semaphore()
    for b in range(bits):
        pl.semaphore_signal(barrier, inc=1, device_id=partner[b], device_id_type=pl.DeviceIdType.MESH)
    for where in neighbours(-1):
        pl.semaphore_signal(barrier, inc=1, device_id=where, device_id_type=pl.DeviceIdType.MESH)
    pl.semaphore_wait(barrier, bits + 3)

    height, breadth, _ = dx_out.shape
    edges = [
        pltpu.make_async_remote_copy(
            src_ref=src, dst_ref=dst, send_sem=e_send.at[n], recv_sem=e_recv.at[n],
            device_id=where, device_id_type=pl.DeviceIdType.MESH)
        for n, (src, dst, where) in enumerate(zip(
            (edge_ref.at[pl.ds(SHIFT, height - SHIFT), pl.ds(breadth, EDGE)],
             edge_ref.at[pl.ds(height, SHIFT), pl.ds(0, breadth)],
             edge_ref.at[pl.ds(height, SHIFT), pl.ds(breadth, EDGE)]),
            (west_in, north_in, corner_in), neighbours(1)))
    ]

    def copy(src, dst, send, recv, b):
        return pltpu.make_async_remote_copy(
            src_ref=src, dst_ref=dst, send_sem=send, recv_sem=recv,
            device_id=partner[b], device_id_type=pl.DeviceIdType.MESH)

    def select(dims, b, value):
        return tuple(value if d == b else slice(None) for d in dims)

    def reduce_copy(i, s):
        order, (start, rows) = orders[i], chunks[i]
        b = order[s]
        dims = sorted(order[s:])
        if s == 0:
            src = grad_ref.at[select(dims, b, 1 - mine[b]) + (pl.ds(start, rows),)]
        else:
            src = held[i][s - 1].at[select(dims, b, 1 - mine[b])]
        return copy(src, held[i][s], rs_send.at[i, s], rs_recv.at[i, s], b)

    def reduce_add(i, s):
        order, (start, rows) = orders[i], chunks[i]
        b = order[s]
        dims = sorted(order[s:])
        if s == 0:
            kept = grad_ref[select(dims, b, mine[b]) + (pl.ds(start, rows),)]
        else:
            kept = held[i][s - 1][select(dims, b, mine[b])]
        held[i][s][...] += kept

    def gather_copy(i, s):
        order, (start, rows) = orders[i], chunks[i]
        known = set(order[s + 1 :])
        index = tuple(slice(None) if d in known else mine[d] for d in range(bits))
        region = new_ref.at[index + (pl.ds(start, rows),)]
        return copy(region, region, ag_send.at[i, s], ag_recv.at[i, s], order[s])

    def table_copy(s):
        return copy(table_out if s else table_ref, table_held.at[s], t_send.at[s], t_recv.at[s], orders[0][s])

    fetch = pltpu.make_async_copy(weight_ref.at[tuple(mine)], own_weight, w_sem)
    fetch.start()
    n = len(chunks)
    live = {}
    for i in range(n):
        live[i] = reduce_copy(i, 0)
        live[i].start()
    table_live = table_copy(0)
    table_live.start()
    for edge in edges:
        edge.start()
    for s in range(bits):
        for i in range(n):
            live[i].wait()
            reduce_add(i, s)
            if s + 1 < bits:
                live[i] = reduce_copy(i, s + 1)
                live[i].start()
            else:
                if i == 0:
                    fetch.wait()
                rows = pl.ds(*chunks[i])
                grad = held[i][s][...] * factor
                first = 0.9 * first_ref[rows] + 0.1 * grad
                second = 0.95 * second_ref[rows] + 0.05 * grad * grad
                first_out[rows] = first
                second_out[rows] = second
                new_ref[tuple(mine) + (rows,)] = own_weight[rows] - 0.01 * first / (jnp.sqrt(second) + 1e-08)
                live[i] = gather_copy(i, s)
                live[i].start()
        table_live.wait()
        if s == 0:
            table_out[...] = table_ref[...] + table_held[s]
        else:
            table_out[...] += table_held[s]
        if s + 1 < bits:
            table_live = table_copy(s + 1)
            table_live.start()
    heads, entries = table_final.shape
    for level in range(-(-entries // LANES)):
        width = min(LANES, entries - level * LANES)
        table_final[:, pl.ds(level * LANES, width)] = (
            table_out[pl.ds(level * HEAD_ROWS, heads), pl.ds(0, width)] * factor
        )
    for edge in edges:
        edge.wait()
    dx_out[SHIFT:, EDGE:] = edge_ref[SHIFT:height, EDGE:breadth]
    dx_out[:SHIFT, EDGE:] = north_in[:, EDGE:]
    column = lax.broadcasted_iota(jnp.int32, (1, EDGE, D), 1)
    dx_out[SHIFT:, :EDGE] = jnp.where(column < SHIFT, west_in[...], edge_ref[SHIFT:height, :EDGE])
    dx_out[:SHIFT, :EDGE] = jnp.where(column < SHIFT, corner_in[...], north_in[:, :EDGE])
    for s in reversed(range(bits)):
        for i in range(n):
            live[i].wait()
            if s > 0:
                live[i] = gather_copy(i, s - 1)
                live[i].start()


def chunk_rows(rows, count):
    groups = -(-rows // 8)
    edges = [min(8 * (groups * i // count), rows) for i in range(count)] + [rows]
    return [(a, b - a) for a, b in zip(edges, edges[1:])]


def reduce_update_gather(grads, table, edge, weights, first, second, table_shape, tile_shape, factor):
    lat_bits, lon_bits = bit_count(lax.axis_size("lat")), bit_count(lax.axis_size("lon"))
    bits = lat_bits + lon_bits
    rows = first.shape[0] // LANES
    chunks = chunk_rows(rows, CHUNKS)
    split_shape = (2,) * bits + (rows, LANES)
    height, breadth, _ = tile_shape
    held = [
        pltpu.VMEM((2,) * (bits - 1 - s) + (count, LANES), F32)
        for _, count in chunks
        for s in range(bits)
    ]
    vmem = pl.BlockSpec(memory_space=pltpu.VMEM)
    shard = jax.ShapeDtypeStruct((rows, LANES), F32)
    dma = pltpu.SemaphoreType.DMA
    new, first_new, second_new, table_sum, dx = pl.pallas_call(
        functools.partial(exchange_kernel, lat_bits, lon_bits, chunks, factor),
        in_specs=[vmem, vmem, vmem, pl.BlockSpec(memory_space=pl.ANY), vmem, vmem],
        out_specs=[vmem] * 5,
        out_shape=[jax.ShapeDtypeStruct(split_shape, F32), shard, shard,
                   jax.ShapeDtypeStruct(table_shape, F32),
                   jax.ShapeDtypeStruct(tile_shape, F32)],
        scratch_shapes=held + [
            pltpu.VMEM((bits,) + table.shape, F32),
            pltpu.VMEM(table.shape, F32),
            pltpu.VMEM((height - SHIFT, EDGE, D), F32),
            pltpu.VMEM((SHIFT, breadth, D), F32),
            pltpu.VMEM((SHIFT, EDGE, D), F32),
            pltpu.VMEM((rows, LANES), F32),
            dma((len(chunks), bits)), dma((len(chunks), bits)),
            dma((len(chunks), bits)), dma((len(chunks), bits)),
            dma((bits,)), dma((bits,)), dma((3,)), dma((3,)), dma(()),
        ],
        compiler_params=pltpu.CompilerParams(
            collective_id=0, has_side_effects=True, vmem_limit_bytes=56 * 1024 * 1024),
    )(grads.reshape(split_shape), table, edge, weights.reshape(split_shape),
      first.reshape(rows, LANES), second.reshape(rows, LANES))
    return new.reshape(-1), first_new.reshape(-1), second_new.reshape(-1), table_sum, dx


def per_device(
    block_input, cotangent, weights, first_moment, second_moment, bias_table, bias_index, region_ids
):
    tile_rows, tile_cols, _ = block_input.shape
    devices = lax.axis_size("lat") * lax.axis_size("lon")
    factor = 1.0 / math.sqrt(tile_rows * tile_cols * devices)
    x, ct = gather_windows(block_input, cotangent)
    grads, edge, table = block_gradients(x, ct, weights, bias_table, bias_index, region_ids)
    gathered, first_new, second_new, table_grad, grad_input = reduce_update_gather(
        grads, table, edge, weights, first_moment, second_moment, bias_table.shape,
        block_input.shape, factor,
    )
    return (grad_input, gathered, first_new, second_new, table_grad)


def solution(mesh):
    placed = (
        P("lat", "lon", None),
        P("lat", "lon", None),
        P(),
        P(("lat", "lon")),
        P(("lat", "lon")),
        P(),
        P(),
        P("lat", "lon"),
    )
    return jax.shard_map(
        per_device,
        mesh=mesh,
        in_specs=placed,
        out_specs=(P("lat", "lon", None), P(), P(("lat", "lon")), P(("lat", "lon")), P()),
        check_vma=False,
    )
```

time: 336 us -> 205 us (0.61); the launches traced: 330 us -> 205 us
  local copies, waits for them, and re-layouts: 73.1 us -> 9.4 us
  matrix products: 41 us -> 0 us
  other arithmetic: 19 us -> 0 us
  starting transfers between devices: 7.07 us -> 0 us
  Pallas kernels: 188 us -> 195 us
    dot_general x11 -> x0, matrix products: 41 us -> none  [dense(): lax.dot_general(a, b, dims, precision=high, preferred_element_type=F32)]
    slice x14 -> x0, local copies, waits for them, and re-layouts: 22.9 us -> none  [the longest x2 8.54 us: unpack(): packed[third_cut:].reshape(FF, D)]
    another operation x14 -> x0, local copies, waits for them, and re-layouts: 13.6 us -> none  [the longest x2 4.22 us: per_device(): x = windows(moved[0]).reshape(tokens, D)]
    reshape x7 -> x0, local copies, waits for them, and re-layouts: 13.5 us -> none  [the longest x4 11.1 us: per_device(): g.reshape(-1)]
    concatenate x4 -> x0, other arithmetic: 11.5 us -> none  [the longest x1 8.87 us: per_device(): jnp.concatenate([g.reshape(-1) for g in (grad_qkv, grad_proj, grad_up, gr...]
    ppermute x4 -> x0, starting transfers between devices: 7.07 us -> none  [passed_along(): lax.ppermute(value, axis, [(i, (i + by) % size) for i in range(size)])]
    transpose x5 -> x0, local copies, waits for them, and re-layouts: 4.52 us -> none  [the longest x3 3.7 us: windows(): return blocks.transpose(0, 2, 1, 3, 4).reshape(-1, WIN * WIN, features)]
    pallas_call x4 -> x2, Pallas kernels: 80.5 us -> 84.6 us  [the longest x1 65.5 us: block_gradients(): pl.pallas_call(block_kernel, in_specs=[vmem] * 6, out_specs=[vmem] * 3, o...]
  transfers between devices with their start and end apart: 4 -> 0, of which waited for: 1 -> 0; matrix products, arithmetic and copies ran while one was open for 13% -> 0% of each run, Pallas kernels for 42% -> 0%
where the time goes in v1:
time: 205 us
  Pallas kernels  195 us (95%)
  local copies, waits for them, and re-layouts  9.4 us (5%)
    pallas_call x1, Pallas kernels, reduce_update_gather(): pl.pallas_call(functools.partial(exchange_kernel, lat_bits, lon_bits, chu...  110 us
    pallas_call x1, Pallas kernels, block_gradients(): pl.pallas_call(block_kernel, in_specs=[vmem] * 6, out_specs=[vmem] * 3, o...  65.5 us
    pallas_call x1, Pallas kernels, gather_windows(): pl.pallas_call(halo_kernel, in_specs=[pl.BlockSpec(memory_space=pl.ANY)]...  19.1 us
    unnamed x11, local copies, waits for them, and re-layouts  9.4 us

profile of v1, /device:TPU:0, one launch (start us, length us, event | category | flops | bytes accessed | tf_op | source)
XLA Modules:
  0.0 204.9 jit_solution(13775522040243065443)
XLA Ops:
  0.6 19.1 %shard_map.119 = (f32[576,384]{1,0:T(8,128)}, f32[576,384]{1,0:T(8,128)}) custom-call(f32[24,24,384]{2,1,0:T(8,128)} %x_ref.1, f32[24,24,384]{2,1,0:T(8,128)} %ct_ref.1), custom_call_target="tpu_custom_call" | custom-call | tf_op jit(solution)/shard_map/pallas_call | solution.py:126
  19.7 65.5 %shard_map.120 = (f32[13824,128]{1,0:T(8,128)}, f32[30,32,384]{2,1,0:T(8,128)}, f32[80,128]{1,0:T(8,128)}) custom-call(f32[576,384]{1,0:T(8,128)} %get-tuple-element.15.x_ref, f32[576,384]{1,0:T(8,128)} %get-tuple-element.16.ct_ref, f32[13824,128]{1,0:T(8,128)} %bitcast.8, f32[12,529]{1,0:T(8,128)} %table_ref.1, s32[144,144]{1,0:T(8,128)} %index_ref.1, ...), custom_call_target="tpu_custom_call" | custom-call | tf_op jit(solution)/shard_map/pallas_call | solution.py:360
  85.3 110.3 %shard_map.121 = (f32[2,2,2,2,2,432,128]{6,5,4,3,2,1,0:T(8,128)}, f32[432,128]{1,0:T(8,128)}, f32[432,128]{1,0:T(8,128)}, f32[12,529]{1,0:T(8,128)}, f32[24,24,384]{2,1,0:T(8,128)}) custom-call(f32[2,2,2,2,2,432,128]{6,5,4,3,2,1,0:T(8,128)} %bitcast.11, f32[80,128]{1,0:T(8,128)} %get-tuple-element.18.table_ref, f32[30,32,384]{2,1,0:T(8,128)} %get-tuple-element.19.edge_ref, ...), custom_call_target="tpu_custom_call" | custom-call | tf_op jit(solution)/shard_map/pallas_call | solution.py:568
  195.5 2.1 %copy.18 = f32[24,24,384]{2,1,0:T(8,128)} copy(f32[24,24,384]{2,1,0:T(8,128)} %get-tuple-element.30) | data formatting | bytes 1769472
  197.7 0.0 copy-start.1
  197.7 0.0 copy-start
  197.7 0.0 copy-start.2
  197.7 5.2 %copy.19 = f32[1769472]{0:T(1024)} copy(f32[1769472]{0:T(1024)} %bitcast.10) | data formatting | bytes 14155776
  202.9 0.0 copy-done.1
  202.9 0.7 copy.20
  203.6 0.0 copy-done
  203.6 0.7 copy.21
  204.3 0.0 copy-done.2
  204.3 0.6 copy.22
Async XLA Ops:
  197.7 5.2 %copy-start.1 = (f32[432,128]{1,0:T(8,128)S(1)}, f32[432,128]{1,0:T(8,128)}, u32[]{:S(2)}) copy-start(f32[432,128]{1,0:T(8,128)} %get-tuple-element.22) | copy-start | bytes 663556
  197.7 5.9 %copy-start = (f32[432,128]{1,0:T(8,128)S(1)}, f32[432,128]{1,0:T(8,128)}, u32[]{:S(2)}) copy-start(f32[432,128]{1,0:T(8,128)} %get-tuple-element.23) | copy-start | bytes 663556
  197.7 6.7 %copy-start.2 = (f32[12,529]{1,0:T(8,128)S(1)}, f32[12,529]{1,0:T(8,128)}, u32[]{:S(2)}) copy-start(f32[12,529]{1,0:T(8,128)} %get-tuple-element.34) | copy-start | bytes 76180

commit v2 on v1

--- a/solution.py
+++ b/solution.py
@@ -20,7 +20,7 @@
 PACK = LANES // HEAD_DIM
 EDGE = 8
 FF_BLOCK = 512
-CHUNKS = 4
+CHUNKS = 7
 SCALE = 1.0 / math.sqrt(HEAD_DIM)
 
 F32 = jnp.float32
@@ -28,6 +28,13 @@
 NN = (((1,), (0,)), ((), ()))
 NT = (((1,), (1,)), ((), ()))
 VMEM_LIMIT = 63 * 1024 * 1024
+
+def neighbours(by):
+    lat_size, lon_size = lax.axis_size("lat"), lax.axis_size("lon")
+    lat = lax.rem(lax.axis_index("lat") + by + lat_size, lat_size)
+    lon = lax.rem(lax.axis_index("lon") + by + lon_size, lon_size)
+    return ({"lon": lon}, {"lat": lat}, {"lat": lat, "lon": lon})
+
 
 def split(value):
     upper = value.astype(BF16)
@@ -91,33 +98,46 @@
                 at += WIN
 
 
-def halo_kernel(x_ref, ct_ref, xw_ref, ctw_ref, wide, send, recv, local):
-    height, breadth, _ = x_ref.shape
+def greet(places):
     barrier = pltpu.get_barrier_semaphore()
-    for where in neighbours(1):
+    for where in places:
         pl.semaphore_signal(barrier, inc=1, device_id=where, device_id_type=pl.DeviceIdType.MESH)
-    pl.semaphore_wait(barrier, 3)
-    copies = []
-    for n, ref in enumerate((x_ref, ct_ref)):
-        parts = (
-            (ref.at[:, pl.ds(0, EDGE)], wide.at[n, pl.ds(0, height), pl.ds(breadth, EDGE)]),
-            (ref.at[pl.ds(0, SHIFT)], wide.at[n, pl.ds(height, SHIFT), pl.ds(0, breadth)]),
-            (ref.at[pl.ds(0, SHIFT), pl.ds(0, EDGE)],
-             wide.at[n, pl.ds(height, SHIFT), pl.ds(breadth, EDGE)]),
-        )
-        for k, ((src, dst), where) in enumerate(zip(parts, neighbours(-1))):
-            copies.append(pltpu.make_async_remote_copy(
-                src_ref=src, dst_ref=dst, send_sem=send.at[n, k], recv_sem=recv.at[n, k],
-                device_id=where, device_id_type=pl.DeviceIdType.MESH))
-        copies.append(pltpu.make_async_copy(
-            ref, wide.at[n, pl.ds(0, height), pl.ds(0, breadth)], local.at[n]))
+    pl.semaphore_wait(barrier, len(places))
+
+
+def halo_copies(n, ref, wide, send, recv, local):
+    height, breadth, _ = ref.shape
+    parts = (
+        (ref.at[:, pl.ds(0, EDGE)], wide.at[n, pl.ds(0, height), pl.ds(breadth, EDGE)]),
+        (ref.at[pl.ds(0, SHIFT)], wide.at[n, pl.ds(height, SHIFT), pl.ds(0, breadth)]),
+        (ref.at[pl.ds(0, SHIFT), pl.ds(0, EDGE)],
+         wide.at[n, pl.ds(height, SHIFT), pl.ds(breadth, EDGE)]),
+    )
+    copies = [
+        pltpu.make_async_remote_copy(
+            src_ref=src, dst_ref=dst, send_sem=send.at[n, k], recv_sem=recv.at[n, k],
+            device_id=where, device_id_type=pl.DeviceIdType.MESH)
+        for k, ((src, dst), where) in enumerate(zip(parts, neighbours(-1)))
+    ]
+    copies.append(pltpu.make_async_copy(
+        ref, wide.at[n, pl.ds(0, height), pl.ds(0, breadth)], local.at[n]))
     for copy in copies:
         copy.start()
+    return copies
+
+
+def assemble(n, copies, shape, wide, out):
     for copy in copies:
         copy.wait()
+    for at, row, col in window_pieces(shape[0], shape[1]):
+        out[at : at + WIN] = wide[n, row, col : col + WIN]
+
+
+def halo_kernel(x_ref, ct_ref, xw_ref, ctw_ref, wide, send, recv, local):
+    greet(neighbours(1))
+    copies = [halo_copies(n, ref, wide, send, recv, local) for n, ref in enumerate((x_ref, ct_ref))]
     for n, out in enumerate((xw_ref, ctw_ref)):
-        for at, row, col in window_pieces(height, breadth):
-            out[at : at + WIN] = wide[n, row, col : col + WIN]
+        assemble(n, copies[n], x_ref.shape, wide, out)
 
 
 def gather_windows(block_input, cotangent):
@@ -136,9 +156,10 @@
     )(block_input, cotangent)
 
 
-def block_kernel(x_ref, ct_ref, w_ref, table_ref, index_ref, region_ref, grad_ref, edge_ref,
-                 table_out, wq, wp, wu, wd, table, index, bias, dbias, prob, xn_s, mn_s, ct_s,
-                 qkv_s, q_s, ctx_s, d_s, turned, acc, labels, dqkv_s, spread):
+def block_steps(x_ref, ct_ref, w_ref, table_ref, index_ref, region_ref, grad_ref, edge_ref,
+                table_out, d_s, wq, wp, wu, wd, table, index, bias, prob, xn_s, mn_s, ct_s,
+                qkv_s, q_s, ctx_s, turned, acc, labels, spread):
+    dbias, dqkv_s = bias, qkv_s
     height, breadth = region_ref.shape
     across = breadth // WIN
     tokens = x_ref.shape[0]
@@ -157,6 +178,7 @@
     def full(ref):
         return ref[0].astype(F32) + ref[1].astype(F32)
 
+    yield
     for dst, start in zip((wq, wp, wu, wd), row_of):
         _, rows, width = dst.shape
         blocks = width // LANES
@@ -193,8 +215,8 @@
     wrapped = (grid_row >= height * lax.axis_size("lat") - SHIFT).astype(jnp.int32)
     labels[...] = (region_ref[...] * 2 + wrapped).astype(F32)
 
-    x = x_ref[...]
-    x_normed, x_inverse = normalize(x)
+    yield
+    x_normed, x_inverse = normalize(x_ref[...])
     put(xn_s, slice(None), x_normed)
     spread[0] = jnp.broadcast_to(x_inverse, (tokens, LANES))
     qkv = dot_nn(pair(xn_s), pair(wq))
@@ -204,7 +226,6 @@
         upper, lower = split(part)
         qkv_s[0, :, j * D : (j + 1) * D] = upper
         qkv_s[1, :, j * D : (j + 1) * D] = lower
-    put(ct_s, slice(None), ct_ref[...])
 
     lane_head = lax.broadcasted_iota(jnp.int32, (TOK, LANES), 1) >> 5
 
@@ -246,6 +267,8 @@
     lax.fori_loop(0, count, forward, 0)
 
     mixed = x_ref[...] + dot_nn(split(ctx_s[...]), pair(wp))
+    yield
+    put(ct_s, slice(None), ct_ref[...])
     m_normed, m_inverse = normalize(mixed)
     put(mn_s, slice(None), m_normed)
     spread[1] = jnp.broadcast_to(m_inverse, (tokens, LANES))
@@ -324,12 +347,15 @@
     blocks = 3 * D // LANES
     for j in range(blocks):
         grad_ref[pl.ds(row_of[0] + j, D, stride=blocks), :] = grad[:, j * LANES : (j + 1) * LANES]
+    yield
     d_normed = dot_nt(pair(dqkv_s), pair(wq))
+    yield
     q_s[...] = acc[...] + normalize_backward(d_normed, x_normed, spread[0][:, :1])
     edge_ref[...] = jnp.zeros_like(edge_ref)
     for at, row, col in window_pieces(height, breadth):
         edge_ref[row, col : col + WIN] = q_s[at : at + WIN]
 
+    yield
     table_acc = jnp.zeros((levels * 2 * HEAD_ROWS, LANES), F32)
 
     def collect(block, total):
@@ -350,12 +376,43 @@
     table_out[...] = total[: levels * HEAD_ROWS] + total[levels * HEAD_ROWS :]
 
 
+def block_kernel(*refs):
+    for _ in block_steps(*refs):
+        pass
+
+
+def block_scratch(tokens, height, breadth, heads, entries):
+    levels = -(-entries // LANES)
+    return [
+        pltpu.VMEM((2, D, 3 * D), BF16),
+        pltpu.VMEM((2, D, D), BF16),
+        pltpu.VMEM((2, D, FF), BF16),
+        pltpu.VMEM((2, FF, D), BF16),
+        pltpu.VMEM((HEAD_ROWS, levels * LANES), F32),
+        pltpu.VMEM((TOK, 2 * LANES), jnp.int32),
+        pltpu.VMEM((heads, TOK, TOK), F32),
+        pltpu.VMEM((2, tokens // TOK * heads, TOK, TOK), BF16),
+        pltpu.VMEM((2, tokens, D), BF16),
+        pltpu.VMEM((2, tokens, D), BF16),
+        pltpu.VMEM((2, tokens, D), BF16),
+        pltpu.VMEM((2, tokens, 3 * D), BF16),
+        pltpu.VMEM((tokens, D), F32),
+        pltpu.VMEM((tokens, D), F32),
+        pltpu.VMEM((2, 2, D, tokens), BF16),
+        pltpu.VMEM((tokens, D), F32),
+        pltpu.VMEM((height, breadth), F32),
+        pltpu.VMEM((2, tokens, LANES), F32),
+    ]
+
+
+def table_rows(entries):
+    return -(-entries // LANES) * HEAD_ROWS
+
+
 def block_gradients(x, ct, weights, bias_table, bias_index, region_ids):
     tokens = x.shape[0]
     height, breadth = region_ids.shape
     heads, entries = bias_table.shape
-    levels = -(-entries // LANES)
-    count = tokens // TOK
     vmem = pl.BlockSpec(memory_space=pltpu.VMEM)
     return pl.pallas_call(
         block_kernel,
@@ -364,31 +421,10 @@
         out_shape=[
             jax.ShapeDtypeStruct((weights.shape[0] // LANES, LANES), F32),
             jax.ShapeDtypeStruct((height + SHIFT, breadth + EDGE, D), F32),
-            jax.ShapeDtypeStruct((levels * HEAD_ROWS, LANES), F32),
+            jax.ShapeDtypeStruct((table_rows(entries), LANES), F32),
         ],
-        scratch_shapes=[
-            pltpu.VMEM((2, D, 3 * D), BF16),
-            pltpu.VMEM((2, D, D), BF16),
-            pltpu.VMEM((2, D, FF), BF16),
-            pltpu.VMEM((2, FF, D), BF16),
-            pltpu.VMEM((HEAD_ROWS, levels * LANES), F32),
-            pltpu.VMEM((TOK, 2 * LANES), jnp.int32),
-            pltpu.VMEM((heads, TOK, TOK), F32),
-            pltpu.VMEM((heads, TOK, TOK), F32),
-            pltpu.VMEM((2, count * heads, TOK, TOK), BF16),
-            pltpu.VMEM((2, tokens, D), BF16),
-            pltpu.VMEM((2, tokens, D), BF16),
-            pltpu.VMEM((2, tokens, D), BF16),
-            pltpu.VMEM((2, tokens, 3 * D), BF16),
-            pltpu.VMEM((tokens, D), F32),
-            pltpu.VMEM((tokens, D), F32),
-            pltpu.VMEM((tokens, D), F32),
-            pltpu.VMEM((2, 2, D, tokens), BF16),
-            pltpu.VMEM((tokens, D), F32),
-            pltpu.VMEM((height, breadth), F32),
-            pltpu.VMEM((2, tokens, 3 * D), BF16),
-            pltpu.VMEM((2, tokens, LANES), F32),
-        ],
+        scratch_shapes=[pltpu.VMEM((tokens, D), F32)]
+        + block_scratch(tokens, height, breadth, heads, entries),
         compiler_params=pltpu.CompilerParams(vmem_limit_bytes=VMEM_LIMIT),
     )(x, ct, weights.reshape(-1, LANES), bias_table, bias_index, region_ids)
 
@@ -397,15 +433,7 @@
     return size.bit_length() - 1
 
 
-def neighbours(by):
-    lat_size, lon_size = lax.axis_size("lat"), lax.axis_size("lon")
-    lat = lax.rem(lax.axis_index("lat") + by + lat_size, lat_size)
-    lon = lax.rem(lax.axis_index("lon") + by + lon_size, lon_size)
-    return ({"lon": lon}, {"lat": lat}, {"lat": lat, "lon": lon})
-
-
-def exchange_kernel(lat_bits, lon_bits, chunks, factor, grad_ref, table_ref, edge_ref, weight_ref,
-                    first_ref, second_ref, new_ref, first_out, second_out, table_final, dx_out, *scratch):
+def bit_partners(lat_bits, lon_bits):
     bits = lat_bits + lon_bits
     lat, lon = lax.axis_index("lat"), lax.axis_index("lon")
     mine, partner = [], []
@@ -419,21 +447,22 @@
             bit = lax.rem(lon // step, 2)
             partner.append({"lat": lat, "lon": lon + step * (1 - 2 * bit)})
         mine.append(bit)
+    return mine, partner
+
+
+def exchange_steps(lat_bits, lon_bits, chunks, factor, grad_ref, table_ref, edge_ref, weight_ref,
+                   first_ref, second_ref, new_ref, first_out, second_out, table_final, dx_out, *scratch):
+    bits = lat_bits + lon_bits
+    mine, partner = bit_partners(lat_bits, lon_bits)
     core, inner = bits - 1, list(range(lat_bits, bits - 1))[::-1]
     ahead, back = list(range(lat_bits))[::-1], list(range(lat_bits))
     orders = [[core] + (ahead if i % 2 == 0 else back) + inner for i in range(len(chunks))]
+    orders[-1] = [core] + inner + ahead
     held = [scratch[i * bits : (i + 1) * bits] for i in range(len(chunks))]
     table_held, table_out = scratch[len(chunks) * bits : len(chunks) * bits + 2]
     west_in, north_in, corner_in, own_weight, rs_send, rs_recv, ag_send, ag_recv, t_send, t_recv, e_send, e_recv, w_sem = scratch[
         len(chunks) * bits + 2 :
     ]
-
-    barrier = pltpu.get_barrier_semaphore()
-    for b in range(bits):
-        pl.semaphore_signal(barrier, inc=1, device_id=partner[b], device_id_type=pl.DeviceIdType.MESH)
-    for where in neighbours(-1):
-        pl.semaphore_signal(barrier, inc=1, device_id=where, device_id_type=pl.DeviceIdType.MESH)
-    pl.semaphore_wait(barrier, bits + 3)
 
     height, breadth, _ = dx_out.shape
     edges = [
@@ -492,10 +521,7 @@
     for i in range(n):
         live[i] = reduce_copy(i, 0)
         live[i].start()
-    table_live = table_copy(0)
-    table_live.start()
-    for edge in edges:
-        edge.start()
+    yield
     for s in range(bits):
         for i in range(n):
             live[i].wait()
@@ -515,6 +541,13 @@
                 new_ref[tuple(mine) + (rows,)] = own_weight[rows] - 0.01 * first / (jnp.sqrt(second) + 1e-08)
                 live[i] = gather_copy(i, s)
                 live[i].start()
+        if s == 0:
+            yield
+            for edge in edges:
+                edge.start()
+            yield
+            table_live = table_copy(0)
+            table_live.start()
         table_live.wait()
         if s == 0:
             table_out[...] = table_ref[...] + table_held[s]
@@ -544,10 +577,104 @@
                 live[i].start()
 
 
+def exchange_kernel(lat_bits, lon_bits, *refs):
+    greet(bit_partners(lat_bits, lon_bits)[1] + list(neighbours(-1)))
+    for _ in exchange_steps(lat_bits, lon_bits, *refs):
+        pass
+
+
 def chunk_rows(rows, count):
     groups = -(-rows // 8)
     edges = [min(8 * (groups * i // count), rows) for i in range(count)] + [rows]
     return [(a, b - a) for a, b in zip(edges, edges[1:])]
+
+
+def exchange_scratch(bits, chunks, rows, table_shape, tile_shape):
+    height, breadth, _ = tile_shape
+    dma = pltpu.SemaphoreType.DMA
+    return [
+        pltpu.VMEM((2,) * (bits - 1 - s) + (count, LANES), F32)
+        for _, count in chunks
+        for s in range(bits)
+    ] + [
+        pltpu.VMEM((bits,) + table_shape, F32),
+        pltpu.VMEM(table_shape, F32),
+        pltpu.VMEM((height - SHIFT, EDGE, D), F32),
+        pltpu.VMEM((SHIFT, breadth, D), F32),
+        pltpu.VMEM((SHIFT, EDGE, D), F32),
+        pltpu.VMEM((rows, LANES), F32),
+        dma((len(chunks), bits)), dma((len(chunks), bits)),
+        dma((len(chunks), bits)), dma((len(chunks), bits)),
+        dma((bits,)), dma((bits,)), dma((3,)), dma((3,)), dma(()),
+    ]
+
+
+def fused_kernel(lat_bits, lon_bits, chunks, factor, n_exchange, x_hbm, ct_hbm, weight_ref, table_ref,
+                 index_ref, region_ref, first_ref, second_ref, new_ref, first_out, second_out,
+                 table_final, dx_out, grad, table_part, xw, ctw, wide, send, recv, local, w_sem, *scratch):
+    greet(bit_partners(lat_bits, lon_bits)[1] + list(neighbours(1)) + list(neighbours(-1)))
+    staged = pltpu.make_async_copy(weight_ref, new_ref, w_sem)
+    staged.start()
+    copies = [halo_copies(n, ref, wide, send, recv, local) for n, ref in enumerate((x_hbm, ct_hbm))]
+    edge = wide.at[0]
+    block = block_steps(xw, ctw, new_ref.reshape(grad.shape), table_ref, index_ref, region_ref, grad,
+                        edge, table_part, xw, *scratch[n_exchange:])
+    exchange = exchange_steps(lat_bits, lon_bits, chunks, factor, grad.reshape(new_ref.shape), table_part,
+                              edge, weight_ref, first_ref, second_ref, new_ref, first_out, second_out,
+                              table_final, dx_out, *scratch[:n_exchange])
+    next(block)
+    staged.wait()
+    next(block)
+    assemble(0, copies[0], x_hbm.shape, wide, xw)
+    next(block)
+    assemble(1, copies[1], x_hbm.shape, wide, ctw)
+    next(block)
+    next(exchange)
+    next(block)
+    next(exchange)
+    next(block)
+    next(exchange)
+    for _ in block:
+        pass
+    for _ in exchange:
+        pass
+
+
+def whole_step(block_input, cotangent, weights, first, second, bias_table, bias_index, region_ids, factor):
+    lat_bits, lon_bits = bit_count(lax.axis_size("lat")), bit_count(lax.axis_size("lon"))
+    bits = lat_bits + lon_bits
+    rows = first.shape[0] // LANES
+    chunks = chunk_rows(rows, CHUNKS)
+    split_shape = (2,) * bits + (rows, LANES)
+    tile_shape = block_input.shape
+    height, breadth, _ = tile_shape
+    tokens = height * breadth
+    heads, entries = bias_table.shape
+    table_shape = (table_rows(entries), LANES)
+    vmem, anywhere = pl.BlockSpec(memory_space=pltpu.VMEM), pl.BlockSpec(memory_space=pl.ANY)
+    shard = jax.ShapeDtypeStruct((rows, LANES), F32)
+    dma = pltpu.SemaphoreType.DMA
+    for_exchange = exchange_scratch(bits, chunks, rows, table_shape, tile_shape)
+    new, first_new, second_new, table_sum, dx = pl.pallas_call(
+        functools.partial(fused_kernel, lat_bits, lon_bits, chunks, factor, len(for_exchange)),
+        in_specs=[anywhere] * 3 + [vmem] * 5,
+        out_specs=[vmem] * 5,
+        out_shape=[jax.ShapeDtypeStruct(split_shape, F32), shard, shard,
+                   jax.ShapeDtypeStruct(bias_table.shape, F32),
+                   jax.ShapeDtypeStruct(tile_shape, F32)],
+        scratch_shapes=[
+            pltpu.VMEM((weights.shape[0] // LANES, LANES), F32),
+            pltpu.VMEM(table_shape, F32),
+            pltpu.VMEM((tokens, D), F32),
+            pltpu.VMEM((tokens, D), F32),
+            pltpu.VMEM((2, height + SHIFT, breadth + EDGE, D), F32),
+            dma((2, 3)), dma((2, 3)), dma((2,)), dma(()),
+        ] + for_exchange + block_scratch(tokens, height, breadth, heads, entries),
+        compiler_params=pltpu.CompilerParams(
+            collective_id=2, has_side_effects=True, vmem_limit_bytes=VMEM_LIMIT),
+    )(block_input, cotangent, weights.reshape(split_shape), bias_table, bias_index, region_ids,
+      first.reshape(rows, LANES), second.reshape(rows, LANES))
+    return new.reshape(-1), first_new.reshape(-1), second_new.reshape(-1), table_sum, dx
 
 
 def reduce_update_gather(grads, table, edge, weights, first, second, table_shape, tile_shape, factor):
@@ -556,15 +683,8 @@
     rows = first.shape[0] // LANES
     chunks = chunk_rows(rows, CHUNKS)
     split_shape = (2,) * bits + (rows, LANES)
-    height, breadth, _ = tile_shape
-    held = [
-        pltpu.VMEM((2,) * (bits - 1 - s) + (count, LANES), F32)
-        for _, count in chunks
-        for s in range(bits)
-    ]
     vmem = pl.BlockSpec(memory_space=pltpu.VMEM)
     shard = jax.ShapeDtypeStruct((rows, LANES), F32)
-    dma = pltpu.SemaphoreType.DMA
     new, first_new, second_new, table_sum, dx = pl.pallas_call(
         functools.partial(exchange_kernel, lat_bits, lon_bits, chunks, factor),
         in_specs=[vmem, vmem, vmem, pl.BlockSpec(memory_space=pl.ANY), vmem, vmem],
@@ -572,17 +692,7 @@
         out_shape=[jax.ShapeDtypeStruct(split_shape, F32), shard, shard,
                    jax.ShapeDtypeStruct(table_shape, F32),
                    jax.ShapeDtypeStruct(tile_shape, F32)],
-        scratch_shapes=held + [
-            pltpu.VMEM((bits,) + table.shape, F32),
-            pltpu.VMEM(table.shape, F32),
-            pltpu.VMEM((height - SHIFT, EDGE, D), F32),
-            pltpu.VMEM((SHIFT, breadth, D), F32),
-            pltpu.VMEM((SHIFT, EDGE, D), F32),
-            pltpu.VMEM((rows, LANES), F32),
-            dma((len(chunks), bits)), dma((len(chunks), bits)),
-            dma((len(chunks), bits)), dma((len(chunks), bits)),
-            dma((bits,)), dma((bits,)), dma((3,)), dma((3,)), dma(()),
-        ],
+        scratch_shapes=exchange_scratch(bits, chunks, rows, table.shape, tile_shape),
         compiler_params=pltpu.CompilerParams(
             collective_id=0, has_side_effects=True, vmem_limit_bytes=56 * 1024 * 1024),
     )(grads.reshape(split_shape), table, edge, weights.reshape(split_shape),
@@ -596,6 +706,12 @@
     tile_rows, tile_cols, _ = block_input.shape
     devices = lax.axis_size("lat") * lax.axis_size("lon")
     factor = 1.0 / math.sqrt(tile_rows * tile_cols * devices)
+    if first_moment.shape[0] % (8 * LANES) == 0:
+        gathered, first_new, second_new, table_grad, grad_input = whole_step(
+            block_input, cotangent, weights, first_moment, second_moment, bias_table, bias_index,
+            region_ids, factor,
+        )
+        return (grad_input, gathered, first_new, second_new, table_grad)
     x, ct = gather_windows(block_input, cotangent)
     grads, edge, table = block_gradients(x, ct, weights, bias_table, bias_index, region_ids)
     gathered, first_new, second_new, table_grad, grad_input = reduce_update_gather(

time: 205 us -> 162 us (0.79)
  Pallas kernels: 195 us -> 151 us
    pallas_call x3 -> x1, Pallas kernels: 195 us -> 151 us  [whole_step(): pl.pallas_call(functools.partial(fused_kernel, lat_bits, lon_bits, chunks...]
where the time goes in v2:
time: 162 us; the launch traced here: 161 us
  Pallas kernels  151 us (93%)
  local copies, waits for them, and re-layouts  9.4 us (6%)
    pallas_call x1, Pallas kernels, whole_step(): pl.pallas_call(functools.partial(fused_kernel, lat_bits, lon_bits, chunks...  151 us
    unnamed x11, local copies, waits for them, and re-layouts  9.4 us

profile of v2, /device:TPU:0, one launch (start us, length us, event | category | flops | bytes accessed | tf_op | source)
XLA Modules:
  0.0 161.2 jit_solution(11324571864264178321)
XLA Ops:
  0.6 151.1 %shard_map.119 = (f32[2,2,2,2,2,432,128]{6,5,4,3,2,1,0:T(8,128)}, f32[432,128]{1,0:T(8,128)}, f32[432,128]{1,0:T(8,128)}, f32[12,529]{1,0:T(8,128)}, f32[24,24,384]{2,1,0:T(8,128)}) custom-call(f32[24,24,384]{2,1,0:T(8,128)} %x_hbm.1, f32[24,24,384]{2,1,0:T(8,128)} %ct_hbm.1, f32[2,2,2,2,2,432,128]{6,5,4,3,2,1,0:T(8,128)} %bitcast.7, f32[12,529]{1,0:T(8,128)} %table_ref.1, ...), custom_call_target="tpu_custom_call" | custom-call | tf_op jit(solution)/shard_map/pallas_call | solution.py:658
  151.8 2.1 %copy.18 = f32[24,24,384]{2,1,0:T(8,128)} copy(f32[24,24,384]{2,1,0:T(8,128)} %get-tuple-element.20) | data formatting | bytes 1769472
  153.9 0.0 copy-start.1
  153.9 0.0 copy-start
  153.9 0.0 copy-start.2
  153.9 5.2 %copy.19 = f32[1769472]{0:T(1024)} copy(f32[1769472]{0:T(1024)} %bitcast.6) | data formatting | bytes 14155776
  159.2 0.0 copy-done.1
  159.2 0.7 copy.20
  159.9 0.0 copy-done
  159.9 0.7 copy.21
  160.6 0.0 copy-done.2
  160.6 0.6 copy.22
Async XLA Ops:
  153.9 5.2 %copy-start.1 = (f32[432,128]{1,0:T(8,128)S(1)}, f32[432,128]{1,0:T(8,128)}, u32[]{:S(2)}) copy-start(f32[432,128]{1,0:T(8,128)} %get-tuple-element.12) | copy-start | bytes 663556
  153.9 5.9 %copy-start = (f32[432,128]{1,0:T(8,128)S(1)}, f32[432,128]{1,0:T(8,128)}, u32[]{:S(2)}) copy-start(f32[432,128]{1,0:T(8,128)} %get-tuple-element.13) | copy-start | bytes 663556
  153.9 6.7 %copy-start.2 = (f32[12,529]{1,0:T(8,128)S(1)}, f32[12,529]{1,0:T(8,128)}, u32[]{:S(2)}) copy-start(f32[12,529]{1,0:T(8,128)} %get-tuple-element.24) | copy-start | bytes 76180

commit v3 on v2

--- a/solution.py
+++ b/solution.py
@@ -20,7 +20,10 @@
 PACK = LANES // HEAD_DIM
 EDGE = 8
 FF_BLOCK = 512
-CHUNKS = 7
+CHUNKS = 5
+SEGMENT = 2
+PACE = (0, 2, 2, 2, 3, 3)
+LATER = (3, 3)
 SCALE = 1.0 / math.sqrt(HEAD_DIM)
 
 F32 = jnp.float32
@@ -172,6 +175,14 @@
         upper, lower = split(value)
         ref[0, rows], ref[1, rows] = upper, lower
 
+    def put_turned(n, value):
+        upper, lower = split(jnp.transpose(value))
+        for j, part in enumerate((upper, upper, lower)):
+            turned[n, :, j * tokens : (j + 1) * tokens] = part
+
+    def weight_grad(n, b):
+        return mul(turned[n], jnp.concatenate([b[0], b[1], b[0]], 0), NN)
+
     def pair(ref, *at):
         return ref[(0,) + at], ref[(1,) + at]
 
@@ -234,7 +245,7 @@
         return tuple(jnp.where(keep, v, jnp.zeros_like(v)) for v in values)
 
     def tile(which, t, rows):
-        cols = slice(which * D + t * LANES, which * D + (t + 1) * LANES)
+        cols = pl.ds(pl.multiple_of(which * D + t * LANES, LANES), LANES)
         return qkv_s[0, rows, cols], qkv_s[1, rows, cols]
 
     def forward(w, carry):
@@ -273,7 +284,7 @@
     put(mn_s, slice(None), m_normed)
     spread[1] = jnp.broadcast_to(m_inverse, (tokens, LANES))
     for n, value in enumerate((m_normed, ct_ref[...])):
-        turned[n, 0], turned[n, 1] = split(jnp.transpose(value))
+        put_turned(n, value)
     acc[...] = jnp.zeros_like(acc)
 
     def feed(f, carry):
@@ -283,11 +294,11 @@
         d_up = split(dot_nt(pair(ct_s), pair(wd, cols)) * slope)
         hidden = split(hidden)
         blocks = FF // LANES
-        grad = dot_rows((turned[0, 0], turned[0, 1]), d_up)
+        grad = weight_grad(0, d_up)
         for j in range(FF_BLOCK // LANES):
             start = row_of[2] + f * (FF_BLOCK // LANES) + j
             grad_ref[pl.ds(start, D, stride=blocks), :] = grad[:, j * LANES : (j + 1) * LANES]
-        grad = jnp.transpose(dot_rows((turned[1, 0], turned[1, 1]), hidden))
+        grad = jnp.transpose(weight_grad(1, hidden))
         blocks = D // LANES
         for j in range(blocks):
             start = row_of[3] + f * (FF_BLOCK * blocks) + j
@@ -296,54 +307,59 @@
         return carry
 
     lax.fori_loop(0, FF // FF_BLOCK, feed, 0)
+    yield
 
     d_mixed = ct_ref[...] + normalize_backward(acc[...], full(mn_s), spread[1][:, :1])
     acc[...] = d_mixed
     d_pair = split(d_mixed)
-    turned[0, 0], turned[0, 1] = split(jnp.transpose(ctx_s[...]))
-    grad = dot_rows((turned[0, 0], turned[0, 1]), d_pair)
+    put_turned(0, ctx_s[...])
+    grad = weight_grad(0, d_pair)
     blocks = D // LANES
     for j in range(blocks):
         grad_ref[pl.ds(row_of[1] + j, D, stride=blocks), :] = grad[:, j * LANES : (j + 1) * LANES]
     d_s[...] = dot_nt(d_pair, pair(wp))
     dbias[...] = jnp.zeros_like(dbias)
-
-    def backward(w, carry):
+    yield
+    tiles = D // LANES
+
+    def backward(unit, carry):
+        w, t = unit // tiles, unit % tiles
         rows = pl.ds(pl.multiple_of(w * TOK, TOK), TOK)
-        for t in range(D // LANES):
-            cols = slice(t * LANES, (t + 1) * LANES)
-            k, v = tile(1, t, rows), tile(2, t, rows)
-            grad = d_s[rows, cols]
-            weighed = grad * ctx_s[rows, cols]
-            g = split(grad)
-            g_turned = split(jnp.transpose(grad))
-            q_turned = split(jnp.transpose(q_s[rows, cols]))
-            dq = jnp.zeros((TOK, LANES), F32)
-            dk, dv = [], []
-            for head in range(PACK):
-                h = t * PACK + head
-                part = slice(head * HEAD_DIM, (head + 1) * HEAD_DIM)
-                upper, lower = prob[0, w * heads + h], prob[1, w * heads + h]
-                dprob = dot_nt(only(head, g), v)
-                delta = jnp.sum(jnp.where(lane_head == head, weighed, 0.0), axis=-1, keepdims=True)
-                dscore = (upper.astype(F32) + lower.astype(F32)) * (dprob - delta)
-                dbias[h] += dscore
-                ds = split(dscore)
-                dq += dot_cols(ds, only(head, k))
-                dk.append(dot_rows((q_turned[0][part], q_turned[1][part]), ds))
-                dv.append(dot_rows((g_turned[0][part], g_turned[1][part]), (upper, lower)))
-            for j, value in enumerate((dq * SCALE, jnp.transpose(jnp.concatenate(dk, 0)),
-                                       jnp.transpose(jnp.concatenate(dv, 0)))):
-                at = slice(j * D + t * LANES, j * D + (t + 1) * LANES)
-                upper, lower = split(value)
-                dqkv_s[0, rows, at], dqkv_s[1, rows, at] = upper, lower
+        cols = pl.ds(pl.multiple_of(t * LANES, LANES), LANES)
+        k, v = tile(1, t, rows), tile(2, t, rows)
+        grad = d_s[rows, cols]
+        weighed = grad * ctx_s[rows, cols]
+        g = split(grad)
+        g_turned = split(jnp.transpose(grad))
+        q_turned = split(jnp.transpose(q_s[rows, cols]))
+        dq = jnp.zeros((TOK, LANES), F32)
+        dk, dv = [], []
+        for head in range(PACK):
+            h = t * PACK + head
+            part = slice(head * HEAD_DIM, (head + 1) * HEAD_DIM)
+            upper, lower = prob[0, w * heads + h], prob[1, w * heads + h]
+            dprob = dot_nt(only(head, g), v)
+            delta = jnp.sum(jnp.where(lane_head == head, weighed, 0.0), axis=-1, keepdims=True)
+            dscore = (upper.astype(F32) + lower.astype(F32)) * (dprob - delta)
+            dbias[h] += dscore
+            ds = split(dscore)
+            dq += dot_cols(ds, only(head, k))
+            dk.append(dot_rows((q_turned[0][part], q_turned[1][part]), ds))
+            dv.append(dot_rows((g_turned[0][part], g_turned[1][part]), (upper, lower)))
+        for j, value in enumerate((dq * SCALE, jnp.transpose(jnp.concatenate(dk, 0)),
+                                   jnp.transpose(jnp.concatenate(dv, 0)))):
+            at = pl.ds(pl.multiple_of(j * D + t * LANES, LANES), LANES)
+            upper, lower = split(value)
+            dqkv_s[0, rows, at], dqkv_s[1, rows, at] = upper, lower
         return carry
 
-    lax.fori_loop(0, count, backward, 0)
+    for unit in range(0, count * tiles, SEGMENT):
+        lax.fori_loop(unit, min(unit + SEGMENT, count * tiles), backward, 0)
+        yield
 
     x_normed = full(xn_s)
-    turned[1, 0], turned[1, 1] = split(jnp.transpose(x_normed))
-    grad = dot_rows((turned[1, 0], turned[1, 1]), pair(dqkv_s))
+    put_turned(1, x_normed)
+    grad = weight_grad(1, pair(dqkv_s))
     blocks = 3 * D // LANES
     for j in range(blocks):
         grad_ref[pl.ds(row_of[0] + j, D, stride=blocks), :] = grad[:, j * LANES : (j + 1) * LANES]
@@ -398,7 +414,7 @@
         pltpu.VMEM((2, tokens, 3 * D), BF16),
         pltpu.VMEM((tokens, D), F32),
         pltpu.VMEM((tokens, D), F32),
-        pltpu.VMEM((2, 2, D, tokens), BF16),
+        pltpu.VMEM((2, D, 3 * tokens), BF16),
         pltpu.VMEM((tokens, D), F32),
         pltpu.VMEM((height, breadth), F32),
         pltpu.VMEM((2, tokens, LANES), F32),
@@ -450,137 +466,224 @@
     return mine, partner
 
 
-def exchange_steps(lat_bits, lon_bits, chunks, factor, grad_ref, table_ref, edge_ref, weight_ref,
-                   first_ref, second_ref, new_ref, first_out, second_out, table_final, dx_out, *scratch):
+class HalfExchange:
+    def __init__(self, side, mine, partner, orders, chunks, factor, grad, held, own_weight, first_ref,
+                 second_ref, new_ref, first_out, second_out, sems):
+        self.side, self.mine, self.partner, self.orders = side, mine, partner, orders
+        self.chunks, self.factor, self.grad, self.held = chunks, factor, grad, held
+        self.own_weight, self.first_ref, self.second_ref = own_weight, first_ref, second_ref
+        self.new_ref, self.first_out, self.second_out = new_ref, first_out, second_out
+        self.sums, self.sent = sems[:2], sems[2:]
+        self.owner, self.other = mine[0] == side, mine[0] != side
+        self.bits = len(mine)
+
+    def copy(self, src, dst, sems, i, s):
+        return pltpu.make_async_remote_copy(
+            src_ref=src, dst_ref=dst, send_sem=sems[0].at[self.side, i, s],
+            recv_sem=sems[1].at[self.side, i, s], device_id=self.partner[self.orders[i][s]],
+            device_id_type=pl.DeviceIdType.MESH)
+
+    def run(self, owners_only, action):
+        if owners_only:
+            pl.when(self.owner)(action)
+        else:
+            action()
+
+    def source(self, i, s, kept):
+        b = self.orders[i][s]
+        if b == 0:
+            return self.held[i][s - 1], ()
+        dims = sorted(d for d in self.orders[i][s:] if d)
+        value = self.mine[b] if kept else 1 - self.mine[b]
+        index = tuple(value if d == b else slice(None) for d in dims)
+        if s == 0:
+            return self.grad, (self.side,) + index + (pl.ds(*self.chunks[i]),)
+        return self.held[i][s - 1], index
+
+    def reduce_copy(self, i, s):
+        ref, index = self.source(i, s, False)
+        return self.copy(ref.at[index] if index else ref, self.held[i][s], self.sums, i, s)
+
+    def reduce_start(self, i, s):
+        def start():
+            self.reduce_copy(i, s).start()
+
+        if self.orders[i][s] == 0:
+            pl.when(self.other)(start)
+        else:
+            self.run(0 in self.orders[i][:s], start)
+
+    def reduce_finish(self, i, s):
+        def add():
+            ref, index = self.source(i, s, True)
+            self.held[i][s][...] += ref[index] if index else ref[...]
+
+        def both():
+            self.reduce_copy(i, s).wait()
+            add()
+
+        def take():
+            self.reduce_copy(i, s).wait_recv()
+            add()
+
+        def given():
+            self.reduce_copy(i, s).wait_send()
+
+        if self.orders[i][s] == 0:
+            pl.when(self.other)(given)
+            pl.when(self.owner)(take)
+        else:
+            self.run(0 in self.orders[i][:s], both)
+        if s + 1 < self.bits:
+            self.reduce_start(i, s + 1)
+        else:
+            pl.when(self.owner)(functools.partial(self.update, i))
+            self.gather_start(i, s)
+
+    def update(self, i):
+        rows = pl.ds(*self.chunks[i])
+        grad = self.held[i][self.bits - 1][...] * self.factor
+        first = 0.9 * self.first_ref[rows] + 0.1 * grad
+        second = 0.95 * self.second_ref[rows] + 0.05 * grad * grad
+        self.first_out[rows] = first
+        self.second_out[rows] = second
+        self.new_ref[(self.side,) + tuple(self.mine[1:]) + (rows,)] = (
+            self.own_weight[rows] - 0.01 * first / (jnp.sqrt(second) + 1e-08))
+
+    def gather_copy(self, i, s):
+        known = self.orders[i][s + 1 :]
+        index = tuple(slice(None) if d in known else self.mine[d] for d in range(1, self.bits))
+        region = self.new_ref.at[(self.side,) + index + (pl.ds(*self.chunks[i]),)]
+        return self.copy(region, region, self.sent, i, s)
+
+    def gather_start(self, i, s):
+        def start():
+            self.gather_copy(i, s).start()
+
+        self.run(0 in self.orders[i][: s + 1], start)
+
+    def gather_finish(self, i, s):
+        def both():
+            self.gather_copy(i, s).wait()
+
+        def given():
+            self.gather_copy(i, s).wait_send()
+
+        def take():
+            self.gather_copy(i, s).wait_recv()
+
+        if self.orders[i][s] == 0:
+            pl.when(self.owner)(given)
+            pl.when(self.other)(take)
+        else:
+            self.run(0 in self.orders[i][:s], both)
+        if s > 0:
+            self.gather_start(i, s - 1)
+
+
+class Edges:
+    def __init__(self, edge_ref, dx_out, landing, sems):
+        self.edge, self.out, self.landing, self.sems = edge_ref, dx_out, landing, sems
+
+    def copies(self):
+        height, breadth, _ = self.out.shape
+        sources = (
+            self.edge.at[pl.ds(SHIFT, height - SHIFT), pl.ds(breadth, EDGE)],
+            self.edge.at[pl.ds(height, SHIFT), pl.ds(0, breadth)],
+            self.edge.at[pl.ds(height, SHIFT), pl.ds(breadth, EDGE)],
+        )
+        return [
+            pltpu.make_async_remote_copy(
+                src_ref=src, dst_ref=dst, send_sem=self.sems[0].at[n], recv_sem=self.sems[1].at[n],
+                device_id=where, device_id_type=pl.DeviceIdType.MESH)
+            for n, (src, dst, where) in enumerate(zip(sources, self.landing, neighbours(1)))
+        ]
+
+    def start(self):
+        for copy in self.copies():
+            copy.start()
+
+    def finish(self):
+        for copy in self.copies():
+            copy.wait()
+        edge, out, (west, north, corner) = self.edge, self.out, self.landing
+        height, breadth, _ = out.shape
+        out[SHIFT:, EDGE:] = edge[SHIFT:height, EDGE:breadth]
+        out[:SHIFT, EDGE:] = north[:, EDGE:]
+        column = lax.broadcasted_iota(jnp.int32, (1, EDGE, D), 1)
+        out[SHIFT:, :EDGE] = jnp.where(column < SHIFT, west[...], edge[SHIFT:height, :EDGE])
+        out[:SHIFT, :EDGE] = jnp.where(column < SHIFT, corner[...], north[:, :EDGE])
+
+
+class TableSum:
+    def __init__(self, part, held, total, final, order, partner, factor, sems):
+        self.part, self.held, self.total, self.final = part, held, total, final
+        self.order, self.partner, self.factor, self.sems = order, partner, factor, sems
+
+    def copy(self, s):
+        return pltpu.make_async_remote_copy(
+            src_ref=self.total if s else self.part, dst_ref=self.held.at[s],
+            send_sem=self.sems[0].at[s], recv_sem=self.sems[1].at[s],
+            device_id=self.partner[self.order[s]], device_id_type=pl.DeviceIdType.MESH)
+
+    def start(self, s):
+        self.copy(s).start()
+
+    def finish(self, s):
+        self.copy(s).wait()
+        self.total[...] = (self.total if s else self.part)[...] + self.held[s]
+        if s + 1 < len(self.order):
+            self.start(s + 1)
+            return
+        heads, entries = self.final.shape
+        for level in range(-(-entries // LANES)):
+            width = min(LANES, entries - level * LANES)
+            self.final[:, pl.ds(level * LANES, width)] = (
+                self.total[pl.ds(level * HEAD_ROWS, heads), pl.ds(0, width)] * self.factor
+            )
+
+
+def exchange_parts(lat_bits, lon_bits, chunks, factor, grad, table_part, edge_ref, weight_ref, first_ref,
+                   second_ref, new_ref, first_out, second_out, table_final, dx_out, *scratch):
     bits = lat_bits + lon_bits
     mine, partner = bit_partners(lat_bits, lon_bits)
-    core, inner = bits - 1, list(range(lat_bits, bits - 1))[::-1]
-    ahead, back = list(range(lat_bits))[::-1], list(range(lat_bits))
-    orders = [[core] + (ahead if i % 2 == 0 else back) + inner for i in range(len(chunks))]
-    orders[-1] = [core] + inner + ahead
-    held = [scratch[i * bits : (i + 1) * bits] for i in range(len(chunks))]
-    table_held, table_out = scratch[len(chunks) * bits : len(chunks) * bits + 2]
-    west_in, north_in, corner_in, own_weight, rs_send, rs_recv, ag_send, ag_recv, t_send, t_recv, e_send, e_recv, w_sem = scratch[
-        len(chunks) * bits + 2 :
+    core, inner, ahead = bits - 1, list(range(lat_bits, bits - 1))[::-1], list(range(lat_bits))[::-1]
+    orders = [[core] + (inner + ahead if i % 2 else ahead + inner) for i in range(len(chunks))]
+    held = [scratch[i * bits : (i + 1) * bits] for i in range(2 * len(chunks))]
+    table_held, table_total, *landing, own_weight = scratch[2 * len(chunks) * bits :][:6]
+    sems = scratch[2 * len(chunks) * bits + 6 :]
+    fetch = pltpu.make_async_copy(weight_ref.at[tuple(mine)], own_weight, sems[8])
+    fetch.start()
+    halves = [
+        HalfExchange(side, mine, partner, orders, chunks, factor, grad,
+                     held[side * len(chunks) : (side + 1) * len(chunks)], own_weight, first_ref,
+                     second_ref, new_ref, first_out, second_out, sems[:4])
+        for side in range(2)
     ]
-
-    height, breadth, _ = dx_out.shape
-    edges = [
-        pltpu.make_async_remote_copy(
-            src_ref=src, dst_ref=dst, send_sem=e_send.at[n], recv_sem=e_recv.at[n],
-            device_id=where, device_id_type=pl.DeviceIdType.MESH)
-        for n, (src, dst, where) in enumerate(zip(
-            (edge_ref.at[pl.ds(SHIFT, height - SHIFT), pl.ds(breadth, EDGE)],
-             edge_ref.at[pl.ds(height, SHIFT), pl.ds(0, breadth)],
-             edge_ref.at[pl.ds(height, SHIFT), pl.ds(breadth, EDGE)]),
-            (west_in, north_in, corner_in), neighbours(1)))
-    ]
-
-    def copy(src, dst, send, recv, b):
-        return pltpu.make_async_remote_copy(
-            src_ref=src, dst_ref=dst, send_sem=send, recv_sem=recv,
-            device_id=partner[b], device_id_type=pl.DeviceIdType.MESH)
-
-    def select(dims, b, value):
-        return tuple(value if d == b else slice(None) for d in dims)
-
-    def reduce_copy(i, s):
-        order, (start, rows) = orders[i], chunks[i]
-        b = order[s]
-        dims = sorted(order[s:])
-        if s == 0:
-            src = grad_ref.at[select(dims, b, 1 - mine[b]) + (pl.ds(start, rows),)]
-        else:
-            src = held[i][s - 1].at[select(dims, b, 1 - mine[b])]
-        return copy(src, held[i][s], rs_send.at[i, s], rs_recv.at[i, s], b)
-
-    def reduce_add(i, s):
-        order, (start, rows) = orders[i], chunks[i]
-        b = order[s]
-        dims = sorted(order[s:])
-        if s == 0:
-            kept = grad_ref[select(dims, b, mine[b]) + (pl.ds(start, rows),)]
-        else:
-            kept = held[i][s - 1][select(dims, b, mine[b])]
-        held[i][s][...] += kept
-
-    def gather_copy(i, s):
-        order, (start, rows) = orders[i], chunks[i]
-        known = set(order[s + 1 :])
-        index = tuple(slice(None) if d in known else mine[d] for d in range(bits))
-        region = new_ref.at[index + (pl.ds(start, rows),)]
-        return copy(region, region, ag_send.at[i, s], ag_recv.at[i, s], order[s])
-
-    def table_copy(s):
-        return copy(table_out if s else table_ref, table_held.at[s], t_send.at[s], t_recv.at[s], orders[0][s])
-
-    fetch = pltpu.make_async_copy(weight_ref.at[tuple(mine)], own_weight, w_sem)
-    fetch.start()
-    n = len(chunks)
-    live = {}
-    for i in range(n):
-        live[i] = reduce_copy(i, 0)
-        live[i].start()
-    yield
+    table = TableSum(table_part, table_held, table_total, table_final, orders[0], partner, factor, sems[4:6])
+    return fetch, halves, Edges(edge_ref, dx_out, landing, sems[6:8]), table
+
+
+def exchange_kernel(lat_bits, lon_bits, chunks, factor, *refs):
+    greet(bit_partners(lat_bits, lon_bits)[1] + list(neighbours(-1)))
+    fetch, (low, high), edges, table = exchange_parts(lat_bits, lon_bits, chunks, factor, *refs)
+    each, bits = range(len(chunks)), lat_bits + lon_bits
+    for half in (high, low):
+        for i in each:
+            half.reduce_start(i, 0)
+    edges.start()
+    table.start(0)
+    fetch.wait()
     for s in range(bits):
-        for i in range(n):
-            live[i].wait()
-            reduce_add(i, s)
-            if s + 1 < bits:
-                live[i] = reduce_copy(i, s + 1)
-                live[i].start()
-            else:
-                if i == 0:
-                    fetch.wait()
-                rows = pl.ds(*chunks[i])
-                grad = held[i][s][...] * factor
-                first = 0.9 * first_ref[rows] + 0.1 * grad
-                second = 0.95 * second_ref[rows] + 0.05 * grad * grad
-                first_out[rows] = first
-                second_out[rows] = second
-                new_ref[tuple(mine) + (rows,)] = own_weight[rows] - 0.01 * first / (jnp.sqrt(second) + 1e-08)
-                live[i] = gather_copy(i, s)
-                live[i].start()
-        if s == 0:
-            yield
-            for edge in edges:
-                edge.start()
-            yield
-            table_live = table_copy(0)
-            table_live.start()
-        table_live.wait()
-        if s == 0:
-            table_out[...] = table_ref[...] + table_held[s]
-        else:
-            table_out[...] += table_held[s]
-        if s + 1 < bits:
-            table_live = table_copy(s + 1)
-            table_live.start()
-    heads, entries = table_final.shape
-    for level in range(-(-entries // LANES)):
-        width = min(LANES, entries - level * LANES)
-        table_final[:, pl.ds(level * LANES, width)] = (
-            table_out[pl.ds(level * HEAD_ROWS, heads), pl.ds(0, width)] * factor
-        )
-    for edge in edges:
-        edge.wait()
-    dx_out[SHIFT:, EDGE:] = edge_ref[SHIFT:height, EDGE:breadth]
-    dx_out[:SHIFT, EDGE:] = north_in[:, EDGE:]
-    column = lax.broadcasted_iota(jnp.int32, (1, EDGE, D), 1)
-    dx_out[SHIFT:, :EDGE] = jnp.where(column < SHIFT, west_in[...], edge_ref[SHIFT:height, :EDGE])
-    dx_out[:SHIFT, :EDGE] = jnp.where(column < SHIFT, corner_in[...], north_in[:, :EDGE])
+        for half in (high, low):
+            for i in each:
+                half.reduce_finish(i, s)
+        table.finish(s)
+    edges.finish()
     for s in reversed(range(bits)):
-        for i in range(n):
-            live[i].wait()
-            if s > 0:
-                live[i] = gather_copy(i, s - 1)
-                live[i].start()
-
-
-def exchange_kernel(lat_bits, lon_bits, *refs):
-    greet(bit_partners(lat_bits, lon_bits)[1] + list(neighbours(-1)))
-    for _ in exchange_steps(lat_bits, lon_bits, *refs):
-        pass
+        for half in (high, low):
+            for i in each:
+                half.gather_finish(i, s)
 
 
 def chunk_rows(rows, count):
@@ -592,9 +695,16 @@
 def exchange_scratch(bits, chunks, rows, table_shape, tile_shape):
     height, breadth, _ = tile_shape
     dma = pltpu.SemaphoreType.DMA
+    lat_bits = bit_count(lax.axis_size("lat"))
+
+    def left(i, s):
+        first_at = bits - 1 if i % 2 else lat_bits
+        return bits - 2 - s + (1 if s >= first_at else 0)
+
     return [
-        pltpu.VMEM((2,) * (bits - 1 - s) + (count, LANES), F32)
-        for _, count in chunks
+        pltpu.VMEM((2,) * left(i, s) + (chunks[i][1], LANES), F32)
+        for _ in range(2)
+        for i in range(len(chunks))
         for s in range(bits)
     ] + [
         pltpu.VMEM((bits,) + table_shape, F32),
@@ -603,10 +713,7 @@
         pltpu.VMEM((SHIFT, breadth, D), F32),
         pltpu.VMEM((SHIFT, EDGE, D), F32),
         pltpu.VMEM((rows, LANES), F32),
-        dma((len(chunks), bits)), dma((len(chunks), bits)),
-        dma((len(chunks), bits)), dma((len(chunks), bits)),
-        dma((bits,)), dma((bits,)), dma((3,)), dma((3,)), dma(()),
-    ]
+    ] + [dma((2, len(chunks), bits))] * 4 + [dma((bits,))] * 2 + [dma((3,))] * 2 + [dma(())]
 
 
 def fused_kernel(lat_bits, lon_bits, chunks, factor, n_exchange, x_hbm, ct_hbm, weight_ref, table_ref,
@@ -619,9 +726,17 @@
     edge = wide.at[0]
     block = block_steps(xw, ctw, new_ref.reshape(grad.shape), table_ref, index_ref, region_ref, grad,
                         edge, table_part, xw, *scratch[n_exchange:])
-    exchange = exchange_steps(lat_bits, lon_bits, chunks, factor, grad.reshape(new_ref.shape), table_part,
-                              edge, weight_ref, first_ref, second_ref, new_ref, first_out, second_out,
-                              table_final, dx_out, *scratch[:n_exchange])
+    fetch, (low, high), edges, table = exchange_parts(
+        lat_bits, lon_bits, chunks, factor, grad.reshape(new_ref.shape), table_part, edge, weight_ref,
+        first_ref, second_ref, new_ref, first_out, second_out, table_final, dx_out, *scratch[:n_exchange])
+    each, bits = range(len(chunks)), lat_bits + lon_bits
+    waiting = [(s, i) for s in range(1, bits) for i in each]
+
+    def advance(count):
+        for s, i in waiting[:count]:
+            high.reduce_finish(i, s)
+        del waiting[:count]
+
     next(block)
     staged.wait()
     next(block)
@@ -629,15 +744,43 @@
     next(block)
     assemble(1, copies[1], x_hbm.shape, wide, ctw)
     next(block)
-    next(exchange)
+    for i in each:
+        high.reduce_start(i, 0)
     next(block)
-    next(exchange)
+    for i in each:
+        high.reduce_finish(i, 0)
+    fetch.wait()
+    units = region_ref.size // TOK * (D // LANES)
+    for n in range(-(-units // SEGMENT)):
+        next(block)
+        advance(PACE[n] if n < len(PACE) else 0)
     next(block)
-    next(exchange)
+    for i in each:
+        low.reduce_start(i, 0)
+    advance(LATER[0])
+    next(block)
+    for i in each:
+        low.reduce_finish(i, 0)
+    advance(LATER[1])
+    next(block)
+    edges.start()
+    advance(len(waiting))
     for _ in block:
         pass
-    for _ in exchange:
-        pass
+    table.start(0)
+    for s in range(1, bits):
+        for i in each:
+            low.reduce_finish(i, s)
+        for i in each:
+            high.gather_finish(i, bits - s)
+        table.finish(s - 1)
+    for i in each:
+        high.gather_finish(i, 0)
+    table.finish(bits - 1)
+    edges.finish()
+    for s in reversed(range(bits)):
+        for i in each:
+            low.gather_finish(i, s)
 
 
 def whole_step(block_input, cotangent, weights, first, second, bias_table, bias_index, region_ids, factor):

time: 162 us -> 158 us (0.975)
  Pallas kernels: 151 us -> 147 us
    pallas_call x1, Pallas kernels: 151 us -> 147 us  [whole_step(): pl.pallas_call(functools.partial(fused_kernel, lat_bits, lon_bits, chunks...]
where the time goes in v3:
time: 158 us; the launch traced here: 157 us
  Pallas kernels  147 us (93%)
  local copies, waits for them, and re-layouts  9.4 us (6%)
    pallas_call x1, Pallas kernels, whole_step(): pl.pallas_call(functools.partial(fused_kernel, lat_bits, lon_bits, chunks...  147 us
    unnamed x11, local copies, waits for them, and re-layouts  9.4 us

profile of v3, /device:TPU:0, one launch (start us, length us, event | category | flops | bytes accessed | tf_op | source)
XLA Modules:
  0.0 157.4 jit_solution(14920321422996990450)
XLA Ops:
  0.6 147.3 %shard_map.119 = (f32[2,2,2,2,2,432,128]{6,5,4,3,2,1,0:T(8,128)}, f32[432,128]{1,0:T(8,128)}, f32[432,128]{1,0:T(8,128)}, f32[12,529]{1,0:T(8,128)}, f32[24,24,384]{2,1,0:T(8,128)}) custom-call(f32[24,24,384]{2,1,0:T(8,128)} %x_hbm.1, f32[24,24,384]{2,1,0:T(8,128)} %ct_hbm.1, f32[2,2,2,2,2,432,128]{6,5,4,3,2,1,0:T(8,128)} %bitcast.7, f32[12,529]{1,0:T(8,128)} %table_ref.1, ...), custom_call_target="tpu_custom_call" | custom-call | tf_op jit(solution)/shard_map/pallas_call | solution.py:801
  148.0 2.1 %copy.18 = f32[24,24,384]{2,1,0:T(8,128)} copy(f32[24,24,384]{2,1,0:T(8,128)} %get-tuple-element.20) | data formatting | bytes 1769472
  150.1 0.0 copy-start.1
  150.1 0.0 copy-start
  150.1 0.0 copy-start.2
  150.1 5.2 %copy.19 = f32[1769472]{0:T(1024)} copy(f32[1769472]{0:T(1024)} %bitcast.6) | data formatting | bytes 14155776
  155.4 0.0 copy-done.1
  155.4 0.7 copy.20
  156.1 0.0 copy-done
  156.1 0.7 copy.21
  156.8 0.0 copy-done.2
  156.8 0.6 copy.22
Async XLA Ops:
  150.1 5.2 %copy-start.1 = (f32[432,128]{1,0:T(8,128)S(1)}, f32[432,128]{1,0:T(8,128)}, u32[]{:S(2)}) copy-start(f32[432,128]{1,0:T(8,128)} %get-tuple-element.12) | copy-start | bytes 663556
  150.1 5.9 %copy-start = (f32[432,128]{1,0:T(8,128)S(1)}, f32[432,128]{1,0:T(8,128)}, u32[]{:S(2)}) copy-start(f32[432,128]{1,0:T(8,128)} %get-tuple-element.13) | copy-start | bytes 663556
  150.1 6.7 %copy-start.2 = (f32[12,529]{1,0:T(8,128)S(1)}, f32[12,529]{1,0:T(8,128)}, u32[]{:S(2)}) copy-start(f32[12,529]{1,0:T(8,128)} %get-tuple-element.24) | copy-start | bytes 76180
